TPU v7x, 32 devices: a whole 2x2x4 slice. The times are simulated.
32 devices in a mesh: dp: 2 (over x), tp: 4 (over z), cp: 4 (over y, core).
Axes of the slice: x: 2, y: 2, z: 4, core: 2. Of those that a mesh axis runs over, the one named last changes fastest.
Arguments:
- hidden: bfloat16 [16, 64, 4096], P('dp'), parts along dimension 0
- prefix_len: int32 [16], P('dp'), parts along dimension 0
- k_cache: bfloat16 [16, 16384, 8, 128], P('dp', 'cp', 'tp'), parts along dimension 0
- v_cache: bfloat16 [16, 16384, 8, 128], P('dp', 'cp', 'tp'), parts along dimension 0
- attn_norm: bfloat16 [4096], replicated
- w_q: bfloat16 [4096, 4096], P(None, 'tp')
- w_k: bfloat16 [4096, 1024], P(None, 'tp')
- w_v: bfloat16 [4096, 1024], P(None, 'tp')
- w_o: bfloat16 [4096, 4096], P('tp')
- q_norm: bfloat16 [128], replicated
- k_norm: bfloat16 [128], replicated
Outputs:
- output 1: bfloat16 [16, 64, 4096], P('dp'), parts along dimension 0
- output 2: bfloat16 [16, 64, 8, 128], P('dp', None, 'tp'), parts along dimension 0
- output 3: bfloat16 [16, 64, 8, 128], P('dp', None, 'tp'), parts along dimension 0
There are 2 independent parts. A program takes and returns all parts, laid end to end along the dimension named above; an argument that names none is the same for every part.
All inputs are finite; a program needn't handle non-finite values.
Results may differ from a plain program's by a relative error of at most 0.00828708.
Values sent between devices are 32-bit elements.
A program may use at most 1 GiB of HBM per device.

v0:
```python
import jax
import jax.numpy as jnp
from jax import lax
from jax.sharding import PartitionSpec as P

HEAD_DIM = 128
MASKED = -1e30


def rms_scale(tensor, norm_gain):
    mean_sq = jnp.mean(jnp.square(tensor), axis=-1, keepdims=True)
    return tensor * lax.rsqrt(mean_sq + 1e-6) * norm_gain


def rope_apply(tensor, positions):
    half_dim = HEAD_DIM // 2
    inv_freq = 1.0 / (1000000.0 ** (jnp.arange(half_dim, dtype=jnp.float32) * 2.0 / HEAD_DIM))
    angles = positions.astype(jnp.float32)[..., None] * inv_freq
    cos_t = jnp.cos(angles)[..., None, :]
    sin_t = jnp.sin(angles)[..., None, :]
    lead_half = tensor[..., :half_dim]
    tail_half = tensor[..., half_dim:]
    return jnp.concatenate([lead_half * cos_t - tail_half * sin_t, tail_half * cos_t + lead_half * sin_t], axis=-1)


def project_new(hidden, attn_norm, w_q, w_k, w_v, q_norm, k_norm, prefix_len):
    n_seq, n_new, d_model = hidden.shape
    kv_count = w_k.shape[1] // HEAD_DIM
    head_count = w_q.shape[1] // HEAD_DIM
    normed = rms_scale(hidden.astype(jnp.float32), attn_norm.astype(jnp.float32)).astype(jnp.bfloat16)
    q_lin = jnp.einsum('bce,ef->bcf', normed, w_q, preferred_element_type=jnp.float32).astype(jnp.bfloat16)
    k_lin = jnp.einsum('bce,ef->bcf', normed, w_k, preferred_element_type=jnp.float32).astype(jnp.bfloat16)
    v_lin = jnp.einsum('bce,ef->bcf', normed, w_v, preferred_element_type=jnp.float32).astype(jnp.bfloat16)
    positions = prefix_len[:, None] + jnp.arange(n_new, dtype=jnp.int32)[None, :]
    q_heads = q_lin.reshape(n_seq, n_new, head_count, HEAD_DIM).astype(jnp.float32)
    k_heads = k_lin.reshape(n_seq, n_new, kv_count, HEAD_DIM).astype(jnp.float32)
    q_rot = rope_apply(rms_scale(q_heads, q_norm.astype(jnp.float32)), positions).astype(jnp.bfloat16)
    k_new = rope_apply(rms_scale(k_heads, k_norm.astype(jnp.float32)), positions).astype(jnp.bfloat16)
    v_new = v_lin.reshape(n_seq, n_new, kv_count, HEAD_DIM)
    q_grp = q_rot.reshape(n_seq, n_new, kv_count, head_count // kv_count, HEAD_DIM)
    return q_grp, k_new, v_new


def attend_partial(q_grp, k_cache, v_cache, k_new, v_new, slot_ok, own_ok):
    score_scale = HEAD_DIM ** -0.5
    s_cache = jnp.einsum('bckgd,bpkd->bkcgp', q_grp, k_cache, preferred_element_type=jnp.float32) * score_scale
    s_cache = jnp.where(slot_ok[:, None, None, None, :], s_cache, MASKED)
    s_own = jnp.einsum('bckgd,bikd->bkcgi', q_grp, k_new, preferred_element_type=jnp.float32) * score_scale
    s_own = jnp.where(own_ok[None, None, :, None, :], s_own, MASKED)
    row_max = jnp.maximum(jnp.max(s_cache, axis=-1), jnp.max(s_own, axis=-1))
    p_cache = jnp.exp(s_cache - row_max[..., None])
    p_own = jnp.exp(s_own - row_max[..., None])
    row_sum = jnp.sum(p_cache, axis=-1) + jnp.sum(p_own, axis=-1)
    weighted = jnp.einsum('bkcgp,bpkd->bkcgd', p_cache.astype(jnp.bfloat16), v_cache, preferred_element_type=jnp.float32)
    weighted = weighted + jnp.einsum('bkcgi,bikd->bkcgd', p_own.astype(jnp.bfloat16), v_new, preferred_element_type=jnp.float32)
    return row_max, row_sum, weighted


def out_partial(attn_out, w_o):
    kv_count = attn_out.shape[1]
    group_size = attn_out.shape[3]
    w_heads = w_o.reshape(kv_count, group_size, HEAD_DIM, w_o.shape[1])
    return jnp.einsum('bkcgd,kgde->bce', attn_out, w_heads, preferred_element_type=jnp.float32)


def solution(mesh):
    def per_device(hidden, prefix_len, k_cache, v_cache, attn_norm, w_q, w_k, w_v, w_o, q_norm, k_norm):
        n_new = hidden.shape[1]
        cache_slots = k_cache.shape[1]
        cp_index = lax.axis_index('cp')
        q_grp, k_new, v_new = project_new(hidden, attn_norm, w_q, w_k, w_v, q_norm, k_norm, prefix_len)
        slot_ids = cp_index * cache_slots + jnp.arange(cache_slots)
        slot_ok = slot_ids[None, :] < prefix_len[:, None]
        new_ids = jnp.arange(n_new)
        own_ok = (new_ids[:, None] >= new_ids[None, :]) & (cp_index == 0)
        row_max, row_sum, weighted = attend_partial(q_grp, k_cache, v_cache, k_new, v_new, slot_ok, own_ok)
        glob_max = lax.pmax(row_max, 'cp')
        factor = jnp.exp(row_max - glob_max)
        total_w, total_sum = lax.psum((weighted * factor[..., None], row_sum * factor), 'cp')
        attn_out = (total_w / total_sum[..., None]).astype(jnp.bfloat16)
        out_proj = lax.psum(out_partial(attn_out, w_o), 'tp')
        block_out = (hidden.astype(jnp.float32) + out_proj).astype(jnp.bfloat16)
        return block_out, k_new, v_new

    cache_spec = P('dp', 'cp', 'tp', None)
    arg_specs = (P('dp', None, None), P('dp'), cache_spec, cache_spec, P(None), P(None, 'tp'), P(None, 'tp'), P(None, 'tp'), P('tp', None), P(None), P(None))
    out_specs = (P('dp', None, None), P('dp', None, 'tp', None), P('dp', None, 'tp', None))
    return jax.shard_map(per_device, mesh=mesh, in_specs=arg_specs, out_specs=out_specs, check_vma=False)
```

profile of v0, /device:TPU:1, one launch (start us, length us, event | category | flops | bytes accessed | tf_op | source)
XLA Modules:
  0.0 504.4 jit_solution(6459103756200074349)
XLA Ops:
  7.3 0.9 convert_element_type.61
  8.1 3.5 fusion.8
  11.7 1.3 fusion.47
  13.3 0.6 multiply_reduce_fusion
  14.1 8.4 %fusion.37 = f32[8,64,1024]{2,1,0:T(8,128)S(1)} fusion(bf16[4096,1024]{1,0:T(8,128)(2,1)} %param.16, bf16[8,64,4096]{2,1,0:T(8,128)(2,1)} %param.11, f32[4096]{0:T(1024)S(1)} %convert_element_type.61, f32[8,64]{1,0:T(8,128)S(1)} %add_rsqrt_fusion.2), kind=kOutput, calls=%fused_computation.41 | convolution fusion | flops 4304404480 | bytes 14698496 | tf_op jit(solution)/shard_map/bce,ef->bcf/dot_general | solution.py:31
  23.0 0.6 fusion.25
  24.1 1.0 multiply_cosine_fusion
  25.4 0.7 fusion.26
  26.2 0.8 subtract_convert_fusion
  27.8 2.6 fusion.29
  30.4 30.0 %fusion = (f32[8,2,64,4]{2,3,1,0:T(4,128)S(1)}, f32[8,2,64,4,4096]{4,2,3,1,0:T(8,128)}) fusion(pred[8,4096]{1,0:T(8,128)(4,1)S(1)} %broadcast_compare_fusion, bf16[8,4096,2,128,1]{3,2,1,0,4:T(2,128)(2,1)} %bitcast.72, bf16[8,64,2,4,64]{4,1,3,2,0:T(8,128)(2,1)S(1)} %bitcast.76, bf16[8,64,2,4,64]{4,1,3,2,0:T(8,128)(2,1)S(1)} %bitcast.74), kind=kOutput, calls=%fused_computation.2 | convolution fusion | flops 4347392000 | bytes 84983808 | tf_op jit(solution)/shard_map/bckgd,bpkd->bkcgp/dot_general | solution.py:46
  60.5 11.4 %pmax.7 = f32[8,2,64,4]{2,3,1,0:T(4,128)S(1)} all-reduce(f32[8,2,64,4]{2,3,1,0:T(4,128)S(1)} %max.9), channel_id=1, replica_groups=mesh['dp'=2,'tp'=4,'cp'=4] {'cp'}, use_global_device_ids=true, to_apply=%region_5.6 | all-reduce | flops 4096 | bytes 32768 | tf_op jit(solution)/shard_map/pmax | solution.py:77
  71.9 33.6 %fusion.1 = (f32[8,2,64,4]{2,3,1,0:T(4,128)S(1)}, bf16[8,2,64,4,4096]{4,2,3,1,0:T(8,128)(2,1)}) fusion(f32[8,2,64,4,4096]{4,2,3,1,0:T(8,128)} %get-tuple-element.28, f32[8,2,64,4]{2,3,1,0:T(4,128)S(1)} %max.9, pred[8,4096]{1,0:T(8,128)(4,1)S(1)} %broadcast_compare_fusion), kind=kLoop, calls=%fused_computation.3 | loop fusion | flops 83881984 | bytes 100728832 | tf_op jit(solution)/shard_map/reduce_sum | solution.py:53
  105.5 0.7 fusion.30
  106.3 4.2 fusion.52
  110.5 0.8 reshape.126
  111.2 24.0 %fusion.3 = f32[8,2,64,4,128]{4,2,1,3,0:T(8,128)S(1)} fusion(bf16[8,2,64,4,4096]{4,2,3,1,0:T(8,128)(2,1)} %get-tuple-element.18, bf16[8,4096,2,128,1]{3,2,1,0,4:T(2,128)(2,1)} %bitcast.85), kind=kOutput, calls=%fused_computation.5 | convolution fusion | flops 4294967296 | bytes 52428800 | tf_op jit(solution)/shard_map/bkcgp,bpkd->bkcgd/dot_general | solution.py:54
  135.3 3.0 add_multiply_fusion
  138.3 11.7 %psum.22 = f32[8,2,64,4]{2,3,1,0:T(4,128)S(1)} all-reduce(f32[8,2,64,4]{2,3,1,0:T(4,128)S(1)} %bitcast.82), channel_id=1, replica_groups=mesh['dp'=2,'tp'=4,'cp'=4] {'cp'}, use_global_device_ids=true, to_apply=%region_9.10 | all-reduce | flops 4096 | bytes 32768 | tf_op jit(solution)/shard_map/psum | solution.py:79
  150.0 40.7 %all-reduce.3.cloned.1.call-done = f32[8,2,64,4,128]{4,2,1,3,0:T(8,128)} async-done(((f32[8,2,64,4,128]{4,2,1,3,0:T(8,128)}), f32[8,2,64,4,128]{4,2,1,3,0:T(8,128)}) %all-reduce.3.cloned.1.call-update) | async-done | bytes 2097168 | tf_op jit(solution)/shard_map/psum | solution.py:79
  190.8 9.7 %fusion.17 = f32[8,64,4096]{2,1,0:T(8,128)} fusion(bf16[2,4,128,4096,1]{3,2,1,0,4:T(8,128)(2,1)} %bitcast.86, f32[8,2,64,4,128]{4,2,1,3,0:T(8,128)} %all-reduce.3.cloned.1.call-done, f32[8,2,64,4]{2,1,3,0:T(2,128)S(1)} %copy.60), kind=kOutput, calls=%fused_computation.22 | convolution fusion | flops 4296015872 | bytes 18890752 | tf_op jit(solution)/shard_map/bkcgd,kgde->bce/dot_general | solution.py:63
  200.5 1.0 copy.63
  201.5 287.9 %all-reduce.5.cloned.1.call-done = f32[8,64,4096]{2,1,0:T(8,128)} async-done(((f32[8,64,4096]{2,1,0:T(8,128)}), f32[8,64,4096]{2,1,0:T(8,128)}) %all-reduce.5.cloned.1.call-update) | async-done | bytes 8388624 | tf_op jit(solution)/shard_map/psum | solution.py:81
  489.4 8.2 %fusion.11 = bf16[8,64,4096]{2,1,0:T(8,128)(2,1)} fusion(f32[8,64,4096]{2,1,0:T(8,128)} %all-reduce.5.cloned.1.call-done, bf16[8,64,4096]{2,1,0:T(8,128)(2,1)} %param.11), kind=kLoop, calls=%fused_computation.16 | loop fusion | flops 6291456 | bytes 16777216 | tf_op jit(solution)/shard_map/convert_element_type | solution.py:82
  (45 shorter events, 2.8 us)
Async XLA Ops:
  7.2 4.5 copy-start
  7.2 183.6 %all-reduce.3.cloned.1.call-start = ((), (), s32[]{:S(2)}) async-start(), calls=%async_computation | async-start | bytes 4194304 | tf_op jit(solution)/shard_map/psum | solution.py:79
  7.2 4.4 copy-start.2
  11.6 2.5 copy-start.4
  11.7 2.4 copy-start.6
  11.7 2.4 copy-start.5
  22.5 1.4 copy-start.7
  71.8 33.6 %copy-start.3 = (f32[8,2,64,4,64]{2,4,3,1,0:T(8,128)S(1)}, f32[8,2,64,4,64]{2,4,3,1,0:T(8,128)}, u32[]{:S(2)}) copy-start(f32[8,2,64,4,64]{2,4,3,1,0:T(8,128)} %get-tuple-element.30) | copy-start | bytes 3145732
  138.3 351.2 %all-reduce.5.cloned.1.call-start = ((), (), s32[]{:S(2)}) async-start(), calls=%async_computation.1 | async-start | bytes 16777216 | tf_op jit(solution)/shard_map/psum | solution.py:81
  489.4 8.2 %copy-start.1 = (bf16[4096,256]{1,0:T(8,128)(2,1)S(1)}, bf16[4096,256]{1,0:T(8,128)(2,1)}, u32[]{:S(2)}) copy-start(bf16[4096,256]{1,0:T(8,128)(2,1)} %param.17) | copy-start | bytes 6291460
Sparse Core Ops, SparseCore 0:
  138.4 52.3 all-reduce.2
  200.7 288.7 all-reduce.4
where the time goes:
time: 506 us; the launch traced here: 504 us
  waiting for transfers between devices  329 us (65%)
  matrix products  83.2 us (16%)
  other arithmetic  51.6 us (10%)
  blocking collectives  23.1 us (5%)
  between operations  14.3 us (3%)
    psum x1, waiting for transfers between devices, per_device(): out_proj = lax.psum(out_partial(attn_out, w_o), 'tp')  288 us
    psum x1, waiting for transfers between devices, per_device(): lax.psum((weighted * factor[..., None], row_sum * factor), 'cp')  40.7 us
    reduce_sum x2, other arithmetic, attend_partial(): row_sum = jnp.sum(p_cache, axis=-1) + jnp.sum(p_own, axis=-1)  34.4 us
    dot_general x1, matrix products, attend_partial(): jnp.einsum('bckgd,bpkd->bkcgp', q_grp, k_cache, preferred_element_type=jn...  30 us
    dot_general x1, matrix products, attend_partial(): jnp.einsum('bkcgp,bpkd->bkcgd', p_cache.astype(jnp.bfloat16), v_cache, pr...  24 us
    psum x1, blocking collectives, per_device(): lax.psum((weighted * factor[..., None], row_sum * factor), 'cp')  11.7 us
    pmax x1, blocking collectives, per_device(): glob_max = lax.pmax(row_max, 'cp')  11.4 us
  transfers between devices with their start and end apart: 2, of which 2 were waited for; matrix products, arithmetic and copies ran while one was open for 0% of the time, Pallas kernels for 0%

commit v1 on v0

v1 whole, which is shorter than its diff:
```python
import functools

import jax
import jax.numpy as jnp
from jax import lax
from jax.experimental import pallas as pl
from jax.experimental.pallas import tpu as pltpu
from jax.sharding import PartitionSpec as P

HEAD_DIM = 128
MASKED = -1e30
EXP2_SCALE = HEAD_DIM**-0.5 * 1.4426950408889634
STAT_ROWS = 264
MESH = pl.DeviceIdType.MESH


def project_kernel(
    x_hbm, gain, wq_hbm, wk_hbm, wv_hbm, q_gain, k_gain, cos_t, sin_t,
    q_out, k_out, v_out, x_buf, h_buf, w_buf, x_sem, w_sem,
):
    rows, d_model = x_buf.shape
    n_q = wq_hbm.shape[1] // 256
    x_copy = pltpu.make_async_copy(x_hbm, x_buf, x_sem)
    x_copy.start()
    w_copies = [
        pltpu.make_async_copy(wq_hbm.at[:, pl.ds(256 * i, 256)], w_buf.at[i], w_sem.at[i]) for i in range(n_q)
    ]
    w_copies.append(pltpu.make_async_copy(wk_hbm, w_buf.at[n_q], w_sem.at[n_q]))
    w_copies.append(pltpu.make_async_copy(wv_hbm, w_buf.at[n_q + 1], w_sem.at[n_q + 1]))
    for copy in w_copies:
        copy.start()
    x_copy.wait()

    def norm_rows(i, carry):
        sel = pl.ds(pl.multiple_of(i * 32, 32), 32)
        x = x_buf[sel, :].astype(jnp.float32)
        mean_sq = jnp.mean(x * x, axis=-1, keepdims=True)
        h_buf[sel, :] = (x * lax.rsqrt(mean_sq + 1e-6) * gain[...]).astype(jnp.bfloat16)
        return carry

    lax.fori_loop(0, rows // 32, norm_rows, 0)

    def head_rope(lin, head_gain):
        mean_sq = jnp.mean(lin * lin, axis=-1, keepdims=True)
        t = lin * lax.rsqrt(mean_sq + 1e-6) * head_gain
        return (t * cos_t[...] + pltpu.roll(t, 64, 1) * sin_t[...]).astype(jnp.bfloat16)

    for i in range(n_q + 2):
        w_copies[i].wait()
        lin = jnp.dot(h_buf[...], w_buf[i], preferred_element_type=jnp.float32).astype(jnp.bfloat16)
        if i == n_q + 1:
            v_out[...] = lin
            continue
        head_gain = q_gain[...] if i < n_q else k_gain[...]
        lin = lin.astype(jnp.float32)
        for u in range(2):
            res = head_rope(lin[:, 128 * u : 128 * u + 128], head_gain)
            if i < n_q:
                q_out[:, 256 * i + 128 * u : 256 * i + 128 * u + 128] = res
            else:
                k_out[:, 128 * u : 128 * u + 128] = res


def project(x2, gain, w_q, w_k, w_v, q_gain, k_gain, cos_t, sin_t):
    rows, d_model = x2.shape
    n_tiles = w_q.shape[1] // 256 + 2
    any_spec = pl.BlockSpec(memory_space=pl.ANY)
    vmem = pl.BlockSpec(memory_space=pltpu.VMEM)
    return pl.pallas_call(
        project_kernel,
        out_shape=(
            jax.ShapeDtypeStruct((rows, w_q.shape[1]), jnp.bfloat16),
            jax.ShapeDtypeStruct((rows, 256), jnp.bfloat16),
            jax.ShapeDtypeStruct((rows, 256), jnp.bfloat16),
        ),
        in_specs=[any_spec, vmem, any_spec, any_spec, any_spec, vmem, vmem, vmem, vmem],
        out_specs=(vmem, vmem, vmem),
        scratch_shapes=[
            pltpu.VMEM((rows, d_model), jnp.bfloat16),
            pltpu.VMEM((rows, d_model), jnp.bfloat16),
            pltpu.VMEM((n_tiles, d_model, 256), jnp.bfloat16),
            pltpu.SemaphoreType.DMA,
            pltpu.SemaphoreType.DMA((n_tiles,)),
        ],
        compiler_params=pltpu.CompilerParams(vmem_limit_bytes=56 * 1024 * 1024),
        cost_estimate=pl.CostEstimate(flops=2 * rows * d_model * 256 * n_tiles, bytes_accessed=20 << 20, transcendentals=0),
        name="project",
    )(x2, gain, w_q, w_k, w_v, q_gain, k_gain, cos_t, sin_t)


def attend_kernel(
    nv_ref, q_ref, k_ref, v_ref, kn_ref, vn_ref, o_ref, qt_ref, s_ref, sn_ref, acc_ref, *, tile,
):
    b = pl.program_id(0)
    n_rows = 2 * nv_ref[b]
    has_new = nv_ref[pl.num_programs(0)]
    n_new = kn_ref.shape[1]
    n_tiles = (n_rows + tile - 1) // tile
    q = q_ref[...]
    for h in range(2):
        blocks = [
            q[th * 32 : th * 32 + 32, (h * 4 + g) * 128 : (h * 4 + g) * 128 + 128]
            for th in range(2)
            for g in range(4)
        ]
        qt_ref[h * 128 : h * 128 + 128, :] = jnp.concatenate(blocks, axis=0).T
    sub16 = lax.broadcasted_iota(jnp.int32, (16, 128), 0) & 1
    even_rows = jnp.where(sub16 == 0, 1.0, 0.0).astype(jnp.bfloat16)
    odd_rows = jnp.where(sub16 == 0, 0.0, 1.0).astype(jnp.bfloat16)
    sub8 = lax.broadcasted_iota(jnp.int32, (8, 256), 0) & 1

    def split_rows(k):
        n = k.shape[0]
        k3 = k.reshape(n // 16, 16, 128)
        return jnp.concatenate(
            [(k3 * even_rows[None]).reshape(n, 128), (k3 * odd_rows[None]).reshape(n, 128)], axis=1
        )

    def split_lanes(v):
        n = v.shape[0]
        lane = lax.broadcasted_iota(jnp.int32, (16, n), 1) & 1
        even = jnp.where(lane == 0, 1.0, 0.0).astype(jnp.bfloat16)
        odd = jnp.where(lane == 0, 0.0, 1.0).astype(jnp.bfloat16)
        vt = v.T.reshape(8, 16, n)
        return jnp.concatenate([(vt * even[None]).reshape(128, n), (vt * odd[None]).reshape(128, n)], axis=0)

    def scores(k):
        return jnp.dot(split_rows(k), qt_ref[...], preferred_element_type=jnp.float32)

    def score_tile(t, top):
        sel = pl.ds(pl.multiple_of(t * tile, tile), tile)
        s = scores(k_ref[0, sel, :])
        row = t * tile + lax.broadcasted_iota(jnp.int32, (tile, 256), 0)
        s = jnp.where(row < n_rows, s, MASKED)
        s_ref[sel, :] = s
        return jnp.maximum(top, jnp.max(s.reshape(tile // 8, 8, 256), axis=0))

    top = lax.fori_loop(0, n_tiles, score_tile, jnp.full((8, 256), MASKED, jnp.float32))

    key = lax.broadcasted_iota(jnp.int32, (n_new, 256), 0) // 2
    col = lax.broadcasted_iota(jnp.int32, (n_new, 256), 1)
    token = (col // 128) * 32 + (col % 32)
    s_new = jnp.where((key <= token) & (has_new > 0), scores(kn_ref[0]), MASKED)
    sn_ref[...] = s_new
    top = jnp.maximum(top, jnp.max(s_new.reshape(n_new // 8, 8, 256), axis=0))
    top0 = jnp.max(jnp.where(sub8 == 0, top, MASKED), axis=0, keepdims=True)
    top1 = jnp.max(jnp.where(sub8 == 0, MASKED, top), axis=0, keepdims=True)
    top = jnp.where(sub8 == 0, top0, top1)

    def weigh(s, v, keep):
        n = s.shape[0]
        p = jnp.exp2((s.reshape(n // 8, 8, 256) - top[None]) * EXP2_SCALE)
        if keep is not None:
            p = jnp.where(keep, p, 0.0)
        total = jnp.sum(p, axis=0)
        out = jnp.dot(split_lanes(v), p.reshape(n, 256).astype(jnp.bfloat16), preferred_element_type=jnp.float32)
        return total, out

    total, out = weigh(sn_ref[...], vn_ref[0], has_new > 0)
    acc_ref[...] = out

    def weigh_tile(t, total):
        sel = pl.ds(pl.multiple_of(t * tile, tile), tile)
        more, out = weigh(s_ref[sel, :], v_ref[0, sel, :], None)
        acc_ref[...] += out
        return total + more

    total = lax.fori_loop(0, n_tiles, weigh_tile, total)
    sum0 = jnp.sum(jnp.where(sub8 == 0, total, 0.0), axis=0, keepdims=True)
    sum1 = jnp.sum(jnp.where(sub8 == 0, 0.0, total), axis=0, keepdims=True)
    stats = jnp.concatenate([top0, top1, sum0, sum1, jnp.zeros((4, 256), jnp.float32)], axis=0)
    for th in range(2):
        o_ref[0, th, 0:256, :] = acc_ref[:, th * 128 : th * 128 + 128]
        o_ref[0, th, 256:264, :] = stats[:, th * 128 : th * 128 + 128]


def attend(n_valid, q2, kc, vc, kn, vn):
    n_seq, cache_rows, _ = kc.shape
    new_rows = kn.shape[1]
    tile = min(2048, cache_rows)
    return pl.pallas_call(
        functools.partial(attend_kernel, tile=tile),
        out_shape=jax.ShapeDtypeStruct((n_seq, 2, STAT_ROWS, 128), jnp.float32),
        grid_spec=pltpu.PrefetchScalarGridSpec(
            num_scalar_prefetch=1,
            grid=(n_seq,),
            in_specs=[
                pl.BlockSpec((q2.shape[0] // n_seq, q2.shape[1]), lambda b, nv: (b, 0)),
                pl.BlockSpec((1, cache_rows, 128), lambda b, nv: (b, 0, 0)),
                pl.BlockSpec((1, cache_rows, 128), lambda b, nv: (b, 0, 0)),
                pl.BlockSpec((1, new_rows, 128), lambda b, nv: (b, 0, 0)),
                pl.BlockSpec((1, new_rows, 128), lambda b, nv: (b, 0, 0)),
            ],
            out_specs=pl.BlockSpec((1, 2, STAT_ROWS, 128), lambda b, nv: (b, 0, 0, 0)),
            scratch_shapes=[
                pltpu.VMEM((256, 256), jnp.bfloat16),
                pltpu.VMEM((cache_rows, 256), jnp.float32),
                pltpu.VMEM((new_rows, 256), jnp.float32),
                pltpu.VMEM((256, 256), jnp.float32),
            ],
        ),
        compiler_params=pltpu.CompilerParams(
            vmem_limit_bytes=56 * 1024 * 1024, dimension_semantics=("arbitrary",)
        ),
        cost_estimate=pl.CostEstimate(
            flops=4 * n_seq * cache_rows * 256 * 256, bytes_accessed=40 << 20, transcendentals=n_seq * cache_rows * 256
        ),
        name="attend",
    )(n_valid, q2, kc, vc, kn, vn)


def finish_kernel(
    part, x_hbm, wo_hbm, out_hbm,
    wo, xs, got1, chip, got2, prod, from_l, from_r, full, stage,
    wo_sem, xs_sem, out_sem, a1s, a1r, a2s, a2r, brs, brr, bls, blr, crs, crr, cls, clr, cys, cyr, cps, cpr,
):
    dp, z, c = lax.axis_index("dp"), lax.axis_index("tp"), lax.axis_index("cp")
    y, core = c // 2, c % 2
    mate = 2 * y + (1 - core)
    over = 2 * (1 - y) + core
    over_mate = 2 * (1 - y) + (1 - core)
    n_chunks, n_part = full.shape[0], full.shape[2]
    width = full.shape[4]
    last = n_part - 1

    def send(src, dst, send_sem, recv_sem, tp, cp):
        copy = pltpu.make_async_remote_copy(
            src_ref=src, dst_ref=dst, send_sem=send_sem, recv_sem=recv_sem, device_id=(dp, tp, cp), device_id_type=MESH
        )
        return copy

    wo_copy = pltpu.make_async_copy(wo_hbm, wo, wo_sem)
    wo_copy.start()
    x_copies = [
        pltpu.make_async_copy(
            x_hbm.at[pl.ds(pl.multiple_of(128 * j + 32 * c, 32), 32), pl.ds(pl.multiple_of(width * z, width), width)],
            xs.at[j],
            xs_sem.at[j],
        )
        for j in range(n_chunks)
    ]
    for copy in x_copies:
        copy.start()

    barrier = pltpu.get_barrier_semaphore()
    for peer in (mate, over):
        pl.semaphore_signal(barrier, inc=1, device_id=(dp, z, peer), device_id_type=MESH)

    @pl.when(z > 0)
    def _():
        pl.semaphore_signal(barrier, inc=1, device_id=(dp, z - 1, c), device_id_type=MESH)

    @pl.when(z < last)
    def _():
        pl.semaphore_signal(barrier, inc=1, device_id=(dp, z + 1, c), device_id_type=MESH)

    @pl.when((z == 0) | (z == last))
    def _():
        pl.semaphore_wait(barrier, 3)

    @pl.when((z > 0) & (z < last))
    def _():
        pl.semaphore_wait(barrier, 4)

    def a1(j):
        return send(part.at[pl.ds(2 * j, 2), 1 - core], got1.at[j], a1s.at[j], a1r.at[j], z, mate)

    def a2(j):
        return send(chip.at[j, 1 - y], got2.at[j], a2s.at[j], a2r.at[j], z, over)

    def b_right(j, p):
        return send(prod.at[j, p], from_l.at[j, p], brs.at[j, p], brr.at[j, p], z + 1, c)

    def b_left(j, p):
        return send(prod.at[j, p], from_r.at[j, p], bls.at[j, p], blr.at[j, p], z - 1, c)

    def c_right(j, p):
        return send(full.at[j, c, p], full.at[j, c, p], crs.at[j, p], crr.at[j, p], z + 1, c)

    def c_left(j, p):
        return send(full.at[j, c, p], full.at[j, c, p], cls.at[j, p], clr.at[j, p], z - 1, c)

    def c_over(j, p):
        return send(full.at[j, c, p], full.at[j, c, p], cys.at[j, p], cyr.at[j, p], z, over)

    def c_over_in(j, p):
        return send(full.at[j, over, p], full.at[j, over, p], cys.at[j, p], cyr.at[j, p], z, over)

    def c_mate(j, q, u, p):
        return send(full.at[j, q, p], full.at[j, q, p], cps.at[j, u, p], cpr.at[j, u, p], z, mate)

    def merge(a, b):
        top_a, top_b = a[256:258], b[256:258]
        top = jnp.maximum(top_a, top_b)
        fa = jnp.exp2((top_a - top) * EXP2_SCALE)
        fb = jnp.exp2((top_b - top) * EXP2_SCALE)
        vals = [
            a[128 * h : 128 * h + 128] * fa[h : h + 1] + b[128 * h : 128 * h + 128] * fb[h : h + 1] for h in range(2)
        ]
        return vals, top, a[258:260] * fa + b[258:260] * fb

    for j in range(n_chunks):
        a1(j).start()

    def stage_a1(j):
        a1(j).wait_recv()
        for s in range(2):
            vals, top, total = merge(part[2 * j + s, core], got1[j, s])
            chip[j, s, 0:128] = vals[0]
            chip[j, s, 128:256] = vals[1]
            chip[j, s, 256:264] = jnp.concatenate([top, total, jnp.zeros((4, 128), jnp.float32)], axis=0)
        a2(j).start()

    def stage_a2(j):
        a2(j).wait_recv()
        vals, _, total = merge(chip[j, y], got2[j])
        turned = [(vals[h] / total[h : h + 1]).T for h in range(2)]
        o = jnp.concatenate([turned[h][32 * g : 32 * g + 32] for h in range(2) for g in range(4)], axis=1)
        o = o.astype(jnp.bfloat16)
        if j == 0:
            wo_copy.wait()

        def one_part(p, carry):
            prod[j, p] = jnp.dot(
                o, wo[:, pl.ds(pl.multiple_of(p * width, width), width)], preferred_element_type=jnp.float32
            )
            return carry

        lax.fori_loop(0, n_part, one_part, 0)

        @pl.when(z == 0)
        def _():
            for p in range(last, 0, -1):
                b_right(j, p).start()

        @pl.when(z == last)
        def _():
            for p in range(last):
                b_left(j, p).start()

    def pass_right(j, p):
        b_right(j, p).wait_recv()
        prod[j, p] = prod[j, p] + from_l[j, p]
        b_right(j, p).start()

    def pass_left(j, p):
        b_left(j, p).wait_recv()
        prod[j, p] = prod[j, p] + from_r[j, p]
        b_left(j, p).start()

    def stage_b1(j):
        @pl.when(z == 1)
        def _():
            pass_right(j, 3)
            pass_right(j, 2)

        @pl.when(z == 2)
        def _():
            pass_left(j, 0)
            pass_left(j, 1)

    def stage_b2(j):
        @pl.when(z == 2)
        def _():
            pass_right(j, 3)

        @pl.when(z == 1)
        def _():
            pass_left(j, 0)

    def stage_c0(j):
        x_copies[j].wait()

        @pl.when(z > 0)
        def _():
            b_right(j, z).wait_recv()
            prod[j, z] = prod[j, z] + from_l[j, z]

        @pl.when(z < last)
        def _():
            b_left(j, z).wait_recv()
            prod[j, z] = prod[j, z] + from_r[j, z]

        full[j, c, z] = prod[j, z] + xs[j].astype(jnp.float32)

        @pl.when(z < last)
        def _():
            c_right(j, z).start()

        @pl.when(z > 0)
        def _():
            c_left(j, z).start()

        c_over(j, z).start()
        c_mate(j, c, 0, z).start()

    def stage_c(j, d):
        @pl.when(z - d >= 0)
        def _():
            p = z - d
            c_right(j, p).wait_recv()

            @pl.when(z < last)
            def _():
                c_right(j, p).start()

            c_over(j, p).start()
            c_mate(j, c, 0, p).start()

        @pl.when(z + d <= last)
        def _():
            p = z + d
            c_left(j, p).wait_recv()

            @pl.when(z > 0)
            def _():
                c_left(j, p).start()

            c_over(j, p).start()
            c_mate(j, c, 0, p).start()

    def stage_over(j):
        for p in range(n_part):
            c_over_in(j, p).wait_recv()
            c_mate(j, over, 1, p).start()

    def out_copy(j):
        return pltpu.make_async_copy(stage.at[j], out_hbm.at[pl.ds(128 * j, 128)], out_sem.at[j])

    def stage_out(j):
        for p in range(n_part):
            c_mate(j, mate, 0, p).wait_recv()
            c_mate(j, over_mate, 1, p).wait_recv()
        for q in range(4):
            for p in range(n_part):
                stage[j, 32 * q : 32 * q + 32, width * p : width * p + width] = full[j, q, p].astype(jnp.bfloat16)
        out_copy(j).start()

    stages = [
        stage_a1, stage_a2, stage_b1, stage_b2, stage_c0,
        functools.partial(stage_c, d=1), functools.partial(stage_c, d=2), functools.partial(stage_c, d=3),
        stage_over, stage_out,
    ]
    for r in range(n_chunks + len(stages) - 1):
        for i, stage_fn in enumerate(stages):
            if 0 <= r - i < n_chunks:
                stage_fn(r - i)

    for j in range(n_chunks):
        a1(j).wait_send()
        a2(j).wait_send()
        for p in range(n_part):
            @pl.when(z < p)
            def _():
                b_right(j, p).wait_send()

            @pl.when(z > p)
            def _():
                b_left(j, p).wait_send()

            @pl.when((z >= p) & (z < last))
            def _():
                c_right(j, p).wait_send()

            @pl.when((z <= p) & (z > 0))
            def _():
                c_left(j, p).wait_send()

            c_over(j, p).wait_send()
            c_mate(j, c, 0, p).wait_send()
            c_mate(j, over, 1, p).wait_send()
        out_copy(j).wait()


def finish(part, x2, w_o):
    rows, d_model = x2.shape
    n_chunks, n_part = rows // 128, 4
    width = d_model // n_part
    any_spec = pl.BlockSpec(memory_space=pl.ANY)
    piece = (32, width)
    f32 = jnp.float32
    sems = pltpu.SemaphoreType.DMA
    per_part = [sems((n_chunks, n_part))] * 10
    return pl.pallas_call(
        finish_kernel,
        out_shape=jax.ShapeDtypeStruct((rows, d_model), jnp.bfloat16),
        in_specs=[pl.BlockSpec(memory_space=pltpu.VMEM), any_spec, any_spec],
        out_specs=any_spec,
        scratch_shapes=[
            pltpu.VMEM(w_o.shape, jnp.bfloat16),
            pltpu.VMEM((n_chunks, *piece), jnp.bfloat16),
            pltpu.VMEM((n_chunks, 2, STAT_ROWS, 128), f32),
            pltpu.VMEM((n_chunks, 2, STAT_ROWS, 128), f32),
            pltpu.VMEM((n_chunks, STAT_ROWS, 128), f32),
            pltpu.VMEM((n_chunks, n_part, *piece), f32),
            pltpu.VMEM((n_chunks, n_part, *piece), f32),
            pltpu.VMEM((n_chunks, n_part, *piece), f32),
            pltpu.VMEM((n_chunks, 4, n_part, *piece), f32),
            pltpu.VMEM((n_chunks, 128, d_model), jnp.bfloat16),
            sems,
            sems((n_chunks,)),
            sems((n_chunks,)),
            *[sems((n_chunks,))] * 4,
            *per_part,
            sems((n_chunks, 2, n_part)),
            sems((n_chunks, 2, n_part)),
        ],
        compiler_params=pltpu.CompilerParams(
            collective_id=0, has_side_effects=True, vmem_limit_bytes=56 * 1024 * 1024
        ),
        cost_estimate=pl.CostEstimate(flops=2 * 128 * 1024 * 4096, bytes_accessed=16 << 20, transcendentals=0),
        name="finish",
    )(part, x2, w_o)


def rope_tables(positions):
    half_dim = HEAD_DIM // 2
    inv_freq = 1.0 / (1000000.0 ** (jnp.arange(half_dim, dtype=jnp.float32) * 2.0 / HEAD_DIM))
    angles = positions.astype(jnp.float32)[..., None] * inv_freq
    cos_t, sin_t = jnp.cos(angles), jnp.sin(angles)
    return jnp.concatenate([cos_t, cos_t], axis=-1), jnp.concatenate([-sin_t, sin_t], axis=-1)


def solution(mesh):
    n_cp = mesh.shape["cp"]

    def per_device(hidden, prefix_len, k_cache, v_cache, attn_norm, w_q, w_k, w_v, w_o, q_norm, k_norm):
        n_seq, n_new, d_model = hidden.shape
        slots = k_cache.shape[1]
        cp_index = lax.axis_index("cp")
        x2 = hidden.reshape(n_seq * n_new, d_model)
        positions = prefix_len[:, None] + jnp.arange(n_new, dtype=jnp.int32)[None, :]
        cos_t, sin_t = rope_tables(positions.reshape(-1))
        q2, k2, v2 = project(
            x2, attn_norm.astype(jnp.float32)[None], w_q, w_k, w_v,
            q_norm.astype(jnp.float32)[None], k_norm.astype(jnp.float32)[None], cos_t, sin_t,
        )
        k_new = k2.reshape(n_seq, n_new, 2, HEAD_DIM)
        v_new = v2.reshape(n_seq, n_new, 2, HEAD_DIM)
        n_valid = jnp.clip(prefix_len - cp_index * slots, 0, slots)
        n_valid = jnp.concatenate([n_valid, (cp_index == n_cp - 1).astype(jnp.int32)[None]])
        part = attend(
            n_valid, q2,
            k_cache.reshape(n_seq, slots * 2, HEAD_DIM), v_cache.reshape(n_seq, slots * 2, HEAD_DIM),
            k_new.reshape(n_seq, n_new * 2, HEAD_DIM), v_new.reshape(n_seq, n_new * 2, HEAD_DIM),
        )
        out = finish(part, x2, w_o)
        return out.reshape(hidden.shape), k_new, v_new

    cache_spec = P("dp", "cp", "tp", None)
    arg_specs = (P("dp", None, None), P("dp"), cache_spec, cache_spec, P(None), P(None, "tp"), P(None, "tp"), P(None, "tp"), P("tp", None), P(None), P(None))
    out_specs = (P("dp", None, None), P("dp", None, "tp", None), P("dp", None, "tp", None))
    return jax.shard_map(per_device, mesh=mesh, in_specs=arg_specs, out_specs=out_specs, check_vma=False)
```

time: 506 us -> 181 us (0.36)
  waiting for transfers between devices: 329 us -> 0 us
  Pallas kernels: 0 us -> 160 us
  matrix products: 83.2 us -> 0 us
  other arithmetic: 51.6 us -> 6.59 us
  blocking collectives: 23.1 us -> 0 us
  between operations: 14.3 us -> 0.67 us
  local copies, waits for them, and re-layouts: 3.47 us -> 11.7 us
    psum x2 -> x0, waiting for transfers between devices: 329 us -> none  [the longest x1 288 us: per_device(): out_proj = lax.psum(out_partial(attn_out, w_o), 'tp')]
    pallas_call x0 -> x3, Pallas kernels: none -> 160 us  [the longest x1 93.1 us: finish(): pl.pallas_call(finish_kernel, out_shape=jax.ShapeDtypeStruct((rows, d_mod...]
    dot_general x8 -> x0, matrix products: 83.2 us -> none  [the longest x1 30 us: attend_partial(): jnp.einsum('bckgd,bpkd->bkcgp', q_grp, k_cache, preferred_element_type=jn...]
    reduce_sum x5 -> x0, other arithmetic: 39.1 us -> none  [the longest x2 34.4 us: attend_partial(): row_sum = jnp.sum(p_cache, axis=-1) + jnp.sum(p_own, axis=-1)]
    psum x1 -> x0, blocking collectives: 11.7 us -> none  [per_device(): lax.psum((weighted * factor[..., None], row_sum * factor), 'cp')]
    pmax x1 -> x0, blocking collectives: 11.4 us -> none  [per_device(): glob_max = lax.pmax(row_max, 'cp')]
    convert_element_type x5 -> x1, other arithmetic: 9.09 us -> 0.73 us  [rope_tables(): angles = positions.astype(jnp.float32)[..., None] * inv_freq]
  transfers between devices with their start and end apart: 2 -> 0, of which waited for: 2 -> 0; matrix products, arithmetic and copies ran while one was open for 0% -> 0% of each run, Pallas kernels for 0% -> 0%
where the time goes in v1:
time: 181 us; the launch traced here: 179 us
  Pallas kernels  160 us (88%)
  local copies, waits for them, and re-layouts  11.7 us (6%)
  other arithmetic  6.59 us (4%)
    pallas_call x1, Pallas kernels, finish(): pl.pallas_call(finish_kernel, out_shape=jax.ShapeDtypeStruct((rows, d_mod...  93.1 us
    pallas_call x1, Pallas kernels, attend(): pl.pallas_call(functools.partial(attend_kernel, tile=tile), out_shape=jax...  39.2 us
    pallas_call x1, Pallas kernels, project(): pl.pallas_call(project_kernel, out_shape=(jax.ShapeDtypeStruct((rows, w_q...  27.6 us
    unnamed x1, local copies, waits for them, and re-layouts  4.7 us

profile of v1, /device:TPU:1, one launch (start us, length us, event | category | flops | bytes accessed | tf_op | source)
XLA Modules:
  0.0 178.8 jit_solution(15654452299056237525)
XLA Ops:
  0.6 0.7 subtract_clamp_fusion
  1.3 0.7 pad_add_fusion.nv_ref
  2.0 1.3 bitcast_convert_fusion
  3.2 0.7 add_convert_fusion
  3.9 0.1 convert_element_type.15
  4.0 1.3 broadcast_in_dim.34
  5.3 1.0 fusion
  6.3 1.0 pad_maximum_fusion
  7.3 27.6 %project.1 = (bf16[512,1024]{1,0:T(8,128)(2,1)}, bf16[512,256]{1,0:T(8,128)(2,1)}, bf16[512,256]{1,0:T(8,128)(2,1)}) custom-call(bf16[512,4096]{1,0:T(8,128)(2,1)} %bitcast.13, f32[1,4096]{1,0:T(1,128)} %bitcast.15, bf16[4096,1024]{1,0:T(8,128)(2,1)} %wq_hbm.1, bf16[4096,256]{1,0:T(8,128)(2,1)} %wk_hbm.1, bf16[4096,256]{1,0:T(8,128)(2,1)} %wv_hbm.1, ...), custom_call_target="tpu_custom_call" | custom-call | flops 6442450944 | bytes 20971520 | tf_op jit(solution)/shard_map/project/pallas_call | solution.py:69
  34.9 1.7 reshape.50
  36.6 1.8 reshape_reshape.6.kn_ref
  38.4 1.7 reshape.51
  40.1 1.7 reshape_reshape.7.vn_ref
  41.8 39.2 %attend.1.part = f32[8,2,264,128]{3,2,1,0:T(8,128)} custom-call(s32[9]{0:T(128)} %pad_add_fusion.nv_ref, bf16[512,1024]{1,0:T(8,128)(2,1)} %get-tuple-element.6.q_ref, bf16[8,8192,128]{2,1,0:T(8,128)(2,1)} %bitcast.16, bf16[8,8192,128]{2,1,0:T(8,128)(2,1)} %bitcast.17, bf16[8,128,128]{2,1,0:T(8,128)(2,1)} %reshape_reshape.6.kn_ref, ...), custom_call_target="tpu_custom_call" | custom-call | flops 17179869184 | bytes 41943040 | tf_op jit(solution)/shard_map/attend/pallas_call | solution.py:181
  81.0 93.1 %finish.1 = bf16[512,4096]{1,0:T(8,128)(2,1)} custom-call(f32[8,2,264,128]{3,2,1,0:T(8,128)} %attend.1.part, bf16[512,4096]{1,0:T(8,128)(2,1)} %bitcast.14, bf16[1024,4096]{1,0:T(8,128)(2,1)} %wo_hbm.1), custom_call_target="tpu_custom_call" | custom-call | flops 1073741824 | bytes 16777216 | tf_op jit(solution)/shard_map/finish/pallas_call | solution.py:484
  174.1 4.7 %copy.15 = bf16[8,64,4096]{2,1,0:T(8,128)(2,1)} copy(bf16[8,64,4096]{2,1,0:T(8,128)(2,1)} %bitcast.12) | data formatting | bytes 8388608
  (1 shorter events, 0.0 us)

commit v2 on v1

--- a/solution.py
+++ b/solution.py
@@ -2,6 +2,7 @@
 
 import jax
 import jax.numpy as jnp
+import numpy as np
 from jax import lax
 from jax.experimental import pallas as pl
 from jax.experimental.pallas import tpu as pltpu
@@ -15,91 +16,136 @@
 
 
 def project_kernel(
-    x_hbm, gain, wq_hbm, wk_hbm, wv_hbm, q_gain, k_gain, cos_t, sin_t,
-    q_out, k_out, v_out, x_buf, h_buf, w_buf, x_sem, w_sem,
+    len_ref, x_hbm, gain, wq_hbm, wk_hbm, wv_hbm, q_gain, k_gain, freq,
+    q_out, k_out, v_out, x_buf, h_buf, w_buf, cos_t, sin_t, turn, x_sem, w_sem,
 ):
     rows, d_model = x_buf.shape
     n_q = wq_hbm.shape[1] // 256
-    x_copy = pltpu.make_async_copy(x_hbm, x_buf, x_sem)
-    x_copy.start()
+    n_seq = len_ref.shape[0]
+    n_new = rows // n_seq
+    piece = rows // 4
+    x_copies = [
+        pltpu.make_async_copy(x_hbm.at[pl.ds(piece * i, piece)], x_buf.at[pl.ds(piece * i, piece)], x_sem.at[i])
+        for i in range(4)
+    ]
+    for copy in x_copies:
+        copy.start()
     w_copies = [
         pltpu.make_async_copy(wq_hbm.at[:, pl.ds(256 * i, 256)], w_buf.at[i], w_sem.at[i]) for i in range(n_q)
     ]
     w_copies.append(pltpu.make_async_copy(wk_hbm, w_buf.at[n_q], w_sem.at[n_q]))
     w_copies.append(pltpu.make_async_copy(wv_hbm, w_buf.at[n_q + 1], w_sem.at[n_q + 1]))
-    for copy in w_copies:
-        copy.start()
-    x_copy.wait()
+
+    lane = lax.broadcasted_iota(jnp.int32, (n_new, 128), 1)
+    token = lax.broadcasted_iota(jnp.int32, (n_new, 128), 0)
+
+    def rope_rows(b, carry):
+        angle = (token + len_ref[b]).astype(jnp.float32) * freq[...]
+        sel = pl.ds(pl.multiple_of(b * n_new, n_new), n_new)
+        cos_t[sel, :] = jnp.cos(angle)
+        sin = jnp.sin(angle)
+        sin_t[sel, :] = jnp.where(lane < 64, -sin, sin)
+        return carry
+
+    lax.fori_loop(0, n_seq, rope_rows, 0)
+    x_gain = gain[...].astype(jnp.float32).reshape(1, d_model)
 
     def norm_rows(i, carry):
         sel = pl.ds(pl.multiple_of(i * 32, 32), 32)
         x = x_buf[sel, :].astype(jnp.float32)
         mean_sq = jnp.mean(x * x, axis=-1, keepdims=True)
-        h_buf[sel, :] = (x * lax.rsqrt(mean_sq + 1e-6) * gain[...]).astype(jnp.bfloat16)
+        h_buf[sel, :] = (x * lax.rsqrt(mean_sq + 1e-6) * x_gain).astype(jnp.bfloat16)
         return carry
 
+    for i in range(4):
+        x_copies[i].wait()
+        if i == 0:
+            for copy in w_copies:
+                copy.start()
     lax.fori_loop(0, rows // 32, norm_rows, 0)
-
-    def head_rope(lin, head_gain):
-        mean_sq = jnp.mean(lin * lin, axis=-1, keepdims=True)
-        t = lin * lax.rsqrt(mean_sq + 1e-6) * head_gain
-        return (t * cos_t[...] + pltpu.roll(t, 64, 1) * sin_t[...]).astype(jnp.bfloat16)
-
-    for i in range(n_q + 2):
-        w_copies[i].wait()
+    q_gain_row = q_gain[...].astype(jnp.float32).reshape(1, 128)
+    k_gain_row = k_gain[...].astype(jnp.float32).reshape(1, 128)
+
+    def one_tile(i, carry):
+        pltpu.make_async_copy(w_buf.at[i], w_buf.at[i], w_sem.at[i]).wait()
         lin = jnp.dot(h_buf[...], w_buf[i], preferred_element_type=jnp.float32).astype(jnp.bfloat16)
-        if i == n_q + 1:
-            v_out[...] = lin
-            continue
-        head_gain = q_gain[...] if i < n_q else k_gain[...]
         lin = lin.astype(jnp.float32)
+        head_gain = jnp.where(i < n_q, q_gain_row, k_gain_row)
         for u in range(2):
-            res = head_rope(lin[:, 128 * u : 128 * u + 128], head_gain)
-            if i < n_q:
-                q_out[:, 256 * i + 128 * u : 256 * i + 128 * u + 128] = res
-            else:
-                k_out[:, 128 * u : 128 * u + 128] = res
-
-
-def project(x2, gain, w_q, w_k, w_v, q_gain, k_gain, cos_t, sin_t):
+            raw = lin[:, 128 * u : 128 * u + 128]
+            mean_sq = jnp.mean(raw * raw, axis=-1, keepdims=True)
+            t = raw * lax.rsqrt(mean_sq + 1e-6) * head_gain
+            t = t * cos_t[...] + pltpu.roll(t, 64, 1) * sin_t[...]
+
+            @pl.when(i < n_q)
+            def _():
+                q_out[i, :, 128 * u : 128 * u + 128] = t.astype(jnp.bfloat16)
+
+            @pl.when(i >= n_q)
+            def _():
+                turn[pl.ds(u, rows, stride=2), :] = jnp.where(i == n_q, t, raw)
+
+        @pl.when(i == n_q)
+        def _():
+            k_out[...] = turn[...].astype(jnp.bfloat16)
+
+        @pl.when(i == n_q + 1)
+        def _():
+            v_out[...] = turn[...].astype(jnp.bfloat16)
+
+        return carry
+
+    lax.fori_loop(0, n_q + 2, one_tile, 0)
+
+
+def project(prefix_len, x2, gain, w_q, w_k, w_v, q_gain, k_gain):
     rows, d_model = x2.shape
-    n_tiles = w_q.shape[1] // 256 + 2
+    n_q = w_q.shape[1] // 256
+    half_dim = HEAD_DIM // 2
+    freq = 1.0 / (1000000.0 ** (np.arange(half_dim, dtype=np.float64) * 2.0 / HEAD_DIM))
+    freq = jnp.asarray(np.concatenate([freq, freq])[None], jnp.float32)
     any_spec = pl.BlockSpec(memory_space=pl.ANY)
     vmem = pl.BlockSpec(memory_space=pltpu.VMEM)
     return pl.pallas_call(
         project_kernel,
         out_shape=(
-            jax.ShapeDtypeStruct((rows, w_q.shape[1]), jnp.bfloat16),
-            jax.ShapeDtypeStruct((rows, 256), jnp.bfloat16),
-            jax.ShapeDtypeStruct((rows, 256), jnp.bfloat16),
+            jax.ShapeDtypeStruct((n_q, rows, 256), jnp.bfloat16),
+            jax.ShapeDtypeStruct((2 * rows, 128), jnp.bfloat16),
+            jax.ShapeDtypeStruct((2 * rows, 128), jnp.bfloat16),
         ),
-        in_specs=[any_spec, vmem, any_spec, any_spec, any_spec, vmem, vmem, vmem, vmem],
+        in_specs=[pl.BlockSpec(memory_space=pltpu.SMEM), any_spec, vmem, any_spec, any_spec, any_spec, vmem, vmem, vmem],
         out_specs=(vmem, vmem, vmem),
         scratch_shapes=[
             pltpu.VMEM((rows, d_model), jnp.bfloat16),
             pltpu.VMEM((rows, d_model), jnp.bfloat16),
-            pltpu.VMEM((n_tiles, d_model, 256), jnp.bfloat16),
-            pltpu.SemaphoreType.DMA,
-            pltpu.SemaphoreType.DMA((n_tiles,)),
+            pltpu.VMEM((n_q + 2, d_model, 256), jnp.bfloat16),
+            pltpu.VMEM((rows, 128), jnp.float32),
+            pltpu.VMEM((rows, 128), jnp.float32),
+            pltpu.VMEM((2 * rows, 128), jnp.float32),
+            pltpu.SemaphoreType.DMA((4,)),
+            pltpu.SemaphoreType.DMA((n_q + 2,)),
         ],
         compiler_params=pltpu.CompilerParams(vmem_limit_bytes=56 * 1024 * 1024),
-        cost_estimate=pl.CostEstimate(flops=2 * rows * d_model * 256 * n_tiles, bytes_accessed=20 << 20, transcendentals=0),
+        cost_estimate=pl.CostEstimate(
+            flops=2 * rows * d_model * 256 * (n_q + 2), bytes_accessed=20 << 20, transcendentals=0
+        ),
         name="project",
-    )(x2, gain, w_q, w_k, w_v, q_gain, k_gain, cos_t, sin_t)
+    )(prefix_len, x2, gain, w_q, w_k, w_v, q_gain, k_gain, freq)
 
 
 def attend_kernel(
-    nv_ref, q_ref, k_ref, v_ref, kn_ref, vn_ref, o_ref, qt_ref, s_ref, sn_ref, acc_ref, *, tile,
+    len_ref, q_ref, k_ref, v_ref, kn_ref, vn_ref, o_ref, qt_ref, s_ref, sn_ref, acc_ref, *, tile, n_cp,
 ):
     b = pl.program_id(0)
-    n_rows = 2 * nv_ref[b]
-    has_new = nv_ref[pl.num_programs(0)]
-    n_new = kn_ref.shape[1]
+    cp = lax.axis_index("cp")
+    slots = k_ref.shape[1] // 2
+    n_rows = 2 * jnp.clip(len_ref[b] - cp * slots, 0, slots)
+    has_new = cp == n_cp - 1
+    n_new = kn_ref.shape[0]
     n_tiles = (n_rows + tile - 1) // tile
-    q = q_ref[...]
     for h in range(2):
         blocks = [
-            q[th * 32 : th * 32 + 32, (h * 4 + g) * 128 : (h * 4 + g) * 128 + 128]
+            q_ref[h * 2 + g // 2, th * 32 : th * 32 + 32, (g % 2) * 128 : (g % 2) * 128 + 128]
             for th in range(2)
             for g in range(4)
         ]
@@ -140,7 +186,7 @@
     key = lax.broadcasted_iota(jnp.int32, (n_new, 256), 0) // 2
     col = lax.broadcasted_iota(jnp.int32, (n_new, 256), 1)
     token = (col // 128) * 32 + (col % 32)
-    s_new = jnp.where((key <= token) & (has_new > 0), scores(kn_ref[0]), MASKED)
+    s_new = jnp.where((key <= token) & has_new, scores(kn_ref[...]), MASKED)
     sn_ref[...] = s_new
     top = jnp.maximum(top, jnp.max(s_new.reshape(n_new // 8, 8, 256), axis=0))
     top0 = jnp.max(jnp.where(sub8 == 0, top, MASKED), axis=0, keepdims=True)
@@ -156,7 +202,7 @@
         out = jnp.dot(split_lanes(v), p.reshape(n, 256).astype(jnp.bfloat16), preferred_element_type=jnp.float32)
         return total, out
 
-    total, out = weigh(sn_ref[...], vn_ref[0], has_new > 0)
+    total, out = weigh(sn_ref[...], vn_ref[...], has_new)
     acc_ref[...] = out
 
     def weigh_tile(t, total):
@@ -174,22 +220,22 @@
         o_ref[0, th, 256:264, :] = stats[:, th * 128 : th * 128 + 128]
 
 
-def attend(n_valid, q2, kc, vc, kn, vn):
+def attend(prefix_len, q3, kc, vc, kn, vn, n_cp):
     n_seq, cache_rows, _ = kc.shape
-    new_rows = kn.shape[1]
+    new_rows = kn.shape[0] // n_seq
     tile = min(2048, cache_rows)
     return pl.pallas_call(
-        functools.partial(attend_kernel, tile=tile),
+        functools.partial(attend_kernel, tile=tile, n_cp=n_cp),
         out_shape=jax.ShapeDtypeStruct((n_seq, 2, STAT_ROWS, 128), jnp.float32),
         grid_spec=pltpu.PrefetchScalarGridSpec(
             num_scalar_prefetch=1,
             grid=(n_seq,),
             in_specs=[
-                pl.BlockSpec((q2.shape[0] // n_seq, q2.shape[1]), lambda b, nv: (b, 0)),
+                pl.BlockSpec((q3.shape[0], q3.shape[1] // n_seq, 256), lambda b, nv: (0, b, 0)),
                 pl.BlockSpec((1, cache_rows, 128), lambda b, nv: (b, 0, 0)),
                 pl.BlockSpec((1, cache_rows, 128), lambda b, nv: (b, 0, 0)),
-                pl.BlockSpec((1, new_rows, 128), lambda b, nv: (b, 0, 0)),
-                pl.BlockSpec((1, new_rows, 128), lambda b, nv: (b, 0, 0)),
+                pl.BlockSpec((new_rows, 128), lambda b, nv: (b, 0)),
+                pl.BlockSpec((new_rows, 128), lambda b, nv: (b, 0)),
             ],
             out_specs=pl.BlockSpec((1, 2, STAT_ROWS, 128), lambda b, nv: (b, 0, 0, 0)),
             scratch_shapes=[
@@ -206,7 +252,7 @@
             flops=4 * n_seq * cache_rows * 256 * 256, bytes_accessed=40 << 20, transcendentals=n_seq * cache_rows * 256
         ),
         name="attend",
-    )(n_valid, q2, kc, vc, kn, vn)
+    )(prefix_len, q3, kc, vc, kn, vn)
 
 
 def finish_kernel(
@@ -513,39 +559,19 @@
     )(part, x2, w_o)
 
 
-def rope_tables(positions):
-    half_dim = HEAD_DIM // 2
-    inv_freq = 1.0 / (1000000.0 ** (jnp.arange(half_dim, dtype=jnp.float32) * 2.0 / HEAD_DIM))
-    angles = positions.astype(jnp.float32)[..., None] * inv_freq
-    cos_t, sin_t = jnp.cos(angles), jnp.sin(angles)
-    return jnp.concatenate([cos_t, cos_t], axis=-1), jnp.concatenate([-sin_t, sin_t], axis=-1)
-
-
 def solution(mesh):
     n_cp = mesh.shape["cp"]
 
     def per_device(hidden, prefix_len, k_cache, v_cache, attn_norm, w_q, w_k, w_v, w_o, q_norm, k_norm):
         n_seq, n_new, d_model = hidden.shape
-        slots = k_cache.shape[1]
-        cp_index = lax.axis_index("cp")
         x2 = hidden.reshape(n_seq * n_new, d_model)
-        positions = prefix_len[:, None] + jnp.arange(n_new, dtype=jnp.int32)[None, :]
-        cos_t, sin_t = rope_tables(positions.reshape(-1))
-        q2, k2, v2 = project(
-            x2, attn_norm.astype(jnp.float32)[None], w_q, w_k, w_v,
-            q_norm.astype(jnp.float32)[None], k_norm.astype(jnp.float32)[None], cos_t, sin_t,
-        )
-        k_new = k2.reshape(n_seq, n_new, 2, HEAD_DIM)
-        v_new = v2.reshape(n_seq, n_new, 2, HEAD_DIM)
-        n_valid = jnp.clip(prefix_len - cp_index * slots, 0, slots)
-        n_valid = jnp.concatenate([n_valid, (cp_index == n_cp - 1).astype(jnp.int32)[None]])
+        q3, k_rows, v_rows = project(prefix_len, x2, attn_norm, w_q, w_k, w_v, q_norm, k_norm)
         part = attend(
-            n_valid, q2,
-            k_cache.reshape(n_seq, slots * 2, HEAD_DIM), v_cache.reshape(n_seq, slots * 2, HEAD_DIM),
-            k_new.reshape(n_seq, n_new * 2, HEAD_DIM), v_new.reshape(n_seq, n_new * 2, HEAD_DIM),
+            prefix_len, q3, k_cache.reshape(n_seq, -1, HEAD_DIM), v_cache.reshape(n_seq, -1, HEAD_DIM), k_rows, v_rows, n_cp
         )
         out = finish(part, x2, w_o)
-        return out.reshape(hidden.shape), k_new, v_new
+        new_shape = (n_seq, n_new, 2, HEAD_DIM)
+        return out.reshape(hidden.shape), k_rows.reshape(new_shape), v_rows.reshape(new_shape)
 
     cache_spec = P("dp", "cp", "tp", None)
     arg_specs = (P("dp", None, None), P("dp"), cache_spec, cache_spec, P(None), P(None, "tp"), P(None, "tp"), P(None, "tp"), P("tp", None), P(None), P(None))

time: 181 us -> 158 us (0.87)
  Pallas kernels: 160 us -> 151 us
  local copies, waits for them, and re-layouts: 11.7 us -> 4.7 us
  other arithmetic: 6.59 us -> 0 us
    pallas_call x2, Pallas kernels: 66.7 us -> 49.4 us  [the longest x1 30.8 us: attend(): pl.pallas_call(functools.partial(attend_kernel, tile=tile, n_cp=n_cp), ou...]
    pallas_call x1, Pallas kernels: 93.1 us -> 102 us  [finish(): pl.pallas_call(finish_kernel, out_shape=jax.ShapeDtypeStruct((rows, d_mod...]
    another operation x2 -> x0, local copies, waits for them, and re-layouts: 3.5 us -> none  [the longest x1 1.76 us: per_device(): k_new.reshape(n_seq, n_new * 2, HEAD_DIM)]
    reshape x2 -> x0, local copies, waits for them, and re-layouts: 3.44 us -> none  [the longest x1 1.72 us: per_device(): k_new = k2.reshape(n_seq, n_new, 2, HEAD_DIM)]
    broadcast_in_dim x2 -> x0, other arithmetic: 2.56 us -> none  [the longest x1 1.3 us: per_device(): attn_norm.astype(jnp.float32)[None]]
where the time goes in v2:
time: 158 us; the launch traced here: 156 us
  Pallas kernels  151 us (96%)
  local copies, waits for them, and re-layouts  4.7 us (3%)
    pallas_call x1, Pallas kernels, finish(): pl.pallas_call(finish_kernel, out_shape=jax.ShapeDtypeStruct((rows, d_mod...  102 us
    pallas_call x1, Pallas kernels, attend(): pl.pallas_call(functools.partial(attend_kernel, tile=tile, n_cp=n_cp), ou...  30.8 us
    pallas_call x1, Pallas kernels, project(): pl.pallas_call(project_kernel, out_shape=(jax.ShapeDtypeStruct((n_q, rows...  18.6 us
    unnamed x1, local copies, waits for them, and re-layouts  4.7 us

profile of v2, /device:TPU:1, one launch (start us, length us, event | category | flops | bytes accessed | tf_op | source)
XLA Modules:
  0.0 156.3 jit_solution(15113010017092540824)
XLA Ops:
  0.6 18.6 %project.1 = (bf16[4,512,256]{2,1,0:T(8,128)(2,1)}, bf16[1024,128]{1,0:T(8,128)(2,1)}, bf16[1024,128]{1,0:T(8,128)(2,1)}) custom-call(s32[8]{0:T(128)} %len_ref.3, bf16[512,4096]{1,0:T(8,128)(2,1)} %bitcast.7, bf16[4096]{0:T(1024)(128)(2,1)} %gain.1, bf16[4096,1024]{1,0:T(8,128)(2,1)} %wq_hbm.1, bf16[4096,256]{1,0:T(8,128)(2,1)} %wk_hbm.1, ...), custom_call_target="tpu_custom_call" | custom-call | flops 6442450944 | bytes 20971520 | tf_op jit(solution)/shard_map/project/pallas_call | solution.py:109
  19.3 30.8 %attend.1.part = f32[8,2,264,128]{3,2,1,0:T(8,128)} custom-call(s32[8]{0:T(128)} %len_ref.3, bf16[4,512,256]{2,1,0:T(8,128)(2,1)} %get-tuple-element.6.q_ref, bf16[8,8192,128]{2,1,0:T(8,128)(2,1)} %bitcast.9, bf16[8,8192,128]{2,1,0:T(8,128)(2,1)} %bitcast.10, bf16[1024,128]{1,0:T(8,128)(2,1)} %get-tuple-element.7.kn_ref, ...), custom_call_target="tpu_custom_call" | custom-call | flops 17179869184 | bytes 41943040 | tf_op jit(solution)/shard_map/attend/pallas_call | solution.py:227
  50.1 101.5 %finish.1 = bf16[512,4096]{1,0:T(8,128)(2,1)} custom-call(f32[8,2,264,128]{3,2,1,0:T(8,128)} %attend.1.part, bf16[512,4096]{1,0:T(8,128)(2,1)} %bitcast.8, bf16[1024,4096]{1,0:T(8,128)(2,1)} %wo_hbm.1), custom_call_target="tpu_custom_call" | custom-call | flops 1073741824 | bytes 16777216 | tf_op jit(solution)/shard_map/finish/pallas_call | solution.py:530
  151.6 4.7 %copy.16 = bf16[8,64,4096]{2,1,0:T(8,128)(2,1)} copy(bf16[8,64,4096]{2,1,0:T(8,128)(2,1)} %bitcast.6) | data formatting | bytes 8388608

commit v3 on v2

v3 whole, which is shorter than its diff:
```python
import functools

import jax
import jax.numpy as jnp
import numpy as np
from jax import lax
from jax.experimental import pallas as pl
from jax.experimental.pallas import tpu as pltpu
from jax.sharding import PartitionSpec as P

HEAD_DIM = 128
MASKED = -1e30
EXP2_SCALE = HEAD_DIM**-0.5 * 1.4426950408889634
MESH = pl.DeviceIdType.MESH


def project_kernel(
    len_ref, x_hbm, gain, wq_hbm, wk_hbm, wv_hbm, q_gain, k_gain, freq,
    q_out, k_out, v_out, x_buf, h_buf, w_buf, cos_t, sin_t, turn, x_sem, w_sem,
):
    rows, d_model = x_buf.shape
    n_q = wq_hbm.shape[1] // 256
    n_seq = len_ref.shape[0]
    n_new = rows // n_seq
    piece = rows // 4
    x_copies = [
        pltpu.make_async_copy(x_hbm.at[pl.ds(piece * i, piece)], x_buf.at[pl.ds(piece * i, piece)], x_sem.at[i])
        for i in range(4)
    ]
    for copy in x_copies:
        copy.start()
    w_copies = [
        pltpu.make_async_copy(wq_hbm.at[:, pl.ds(256 * i, 256)], w_buf.at[i], w_sem.at[i]) for i in range(n_q)
    ]
    w_copies.append(pltpu.make_async_copy(wk_hbm, w_buf.at[n_q], w_sem.at[n_q]))
    w_copies.append(pltpu.make_async_copy(wv_hbm, w_buf.at[n_q + 1], w_sem.at[n_q + 1]))

    lane = lax.broadcasted_iota(jnp.int32, (n_new, 128), 1)
    token = lax.broadcasted_iota(jnp.int32, (n_new, 128), 0)

    def rope_rows(b, carry):
        angle = (token + len_ref[b]).astype(jnp.float32) * freq[...]
        sel = pl.ds(pl.multiple_of(b * n_new, n_new), n_new)
        cos_t[sel, :] = jnp.cos(angle)
        sin = jnp.sin(angle)
        sin_t[sel, :] = jnp.where(lane < 64, -sin, sin)
        return carry

    lax.fori_loop(0, n_seq, rope_rows, 0)
    x_gain = gain[...].astype(jnp.float32).reshape(1, d_model)

    def norm_rows(i, carry):
        sel = pl.ds(pl.multiple_of(i * 32, 32), 32)
        x = x_buf[sel, :].astype(jnp.float32)
        mean_sq = jnp.mean(x * x, axis=-1, keepdims=True)
        h_buf[sel, :] = (x * lax.rsqrt(mean_sq + 1e-6) * x_gain).astype(jnp.bfloat16)
        return carry

    for i in range(4):
        x_copies[i].wait()
        if i == 0:
            for copy in w_copies:
                copy.start()
    lax.fori_loop(0, rows // 32, norm_rows, 0)
    q_gain_row = q_gain[...].astype(jnp.float32).reshape(1, 128)
    k_gain_row = k_gain[...].astype(jnp.float32).reshape(1, 128)

    def one_tile(i, carry):
        pltpu.make_async_copy(w_buf.at[i], w_buf.at[i], w_sem.at[i]).wait()
        lin = jnp.dot(h_buf[...], w_buf[i], preferred_element_type=jnp.float32).astype(jnp.bfloat16)
        lin = lin.astype(jnp.float32)
        head_gain = jnp.where(i < n_q, q_gain_row, k_gain_row)
        for u in range(2):
            raw = lin[:, 128 * u : 128 * u + 128]
            mean_sq = jnp.mean(raw * raw, axis=-1, keepdims=True)
            t = raw * lax.rsqrt(mean_sq + 1e-6) * head_gain
            t = t * cos_t[...] + pltpu.roll(t, 64, 1) * sin_t[...]

            @pl.when(i < n_q)
            def _():
                q_out[i, :, 128 * u : 128 * u + 128] = t.astype(jnp.bfloat16)

            @pl.when(i >= n_q)
            def _():
                turn[pl.ds(u, rows, stride=2), :] = jnp.where(i == n_q, t, raw)

        @pl.when(i == n_q)
        def _():
            k_out[...] = turn[...].astype(jnp.bfloat16)

        @pl.when(i == n_q + 1)
        def _():
            v_out[...] = turn[...].astype(jnp.bfloat16)

        return carry

    lax.fori_loop(0, n_q + 2, one_tile, 0)


def project(prefix_len, x2, gain, w_q, w_k, w_v, q_gain, k_gain):
    rows, d_model = x2.shape
    n_q = w_q.shape[1] // 256
    half_dim = HEAD_DIM // 2
    freq = 1.0 / (1000000.0 ** (np.arange(half_dim, dtype=np.float64) * 2.0 / HEAD_DIM))
    freq = jnp.asarray(np.concatenate([freq, freq])[None], jnp.float32)
    any_spec = pl.BlockSpec(memory_space=pl.ANY)
    vmem = pl.BlockSpec(memory_space=pltpu.VMEM)
    return pl.pallas_call(
        project_kernel,
        out_shape=(
            jax.ShapeDtypeStruct((n_q, rows, 256), jnp.bfloat16),
            jax.ShapeDtypeStruct((2 * rows, 128), jnp.bfloat16),
            jax.ShapeDtypeStruct((2 * rows, 128), jnp.bfloat16),
        ),
        in_specs=[pl.BlockSpec(memory_space=pltpu.SMEM), any_spec, vmem, any_spec, any_spec, any_spec, vmem, vmem, vmem],
        out_specs=(vmem, vmem, vmem),
        scratch_shapes=[
            pltpu.VMEM((rows, d_model), jnp.bfloat16),
            pltpu.VMEM((rows, d_model), jnp.bfloat16),
            pltpu.VMEM((n_q + 2, d_model, 256), jnp.bfloat16),
            pltpu.VMEM((rows, 128), jnp.float32),
            pltpu.VMEM((rows, 128), jnp.float32),
            pltpu.VMEM((2 * rows, 128), jnp.float32),
            pltpu.SemaphoreType.DMA((4,)),
            pltpu.SemaphoreType.DMA((n_q + 2,)),
        ],
        compiler_params=pltpu.CompilerParams(vmem_limit_bytes=56 * 1024 * 1024),
        cost_estimate=pl.CostEstimate(
            flops=2 * rows * d_model * 256 * (n_q + 2), bytes_accessed=20 << 20, transcendentals=0
        ),
        name="project",
    )(prefix_len, x2, gain, w_q, w_k, w_v, q_gain, k_gain, freq)


def block_kernel(
    len_ref, q_ref, kn_ref, vn_ref, kc_hbm, vc_hbm, x_hbm, wo_hbm, out_hbm,
    kbuf, vbuf, qt, s_buf, sn_buf, acc, top_buf,
    wo, xs, part, got1, chip, got2, ob, prod, from_l, from_r, full, stage,
    k_sem, v_sem, wo_sem, xs_sem, out_sem, a1s, a1r, a2s, a2r, a3s, a3r,
    brs, brr, bls, blr, crs, crr, cls, clr, cys, cyr, cps, cpr, *, tile,
):
    dp, z, c = lax.axis_index("dp"), lax.axis_index("tp"), lax.axis_index("cp")
    y, core = c // 2, c % 2
    mate = 2 * y + (1 - core)
    over = 2 * (1 - y) + core
    over_mate = 2 * (1 - y) + (1 - core)
    n_seq, n_part, width = full.shape[0], full.shape[2], full.shape[4]
    last = n_part - 1
    cache_rows = kbuf.shape[1]
    n_new = kn_ref.shape[0] // n_seq
    n_tiles = cache_rows // tile

    def send(src, dst, send_sem, recv_sem, tp, cp):
        return pltpu.make_async_remote_copy(
            src_ref=src, dst_ref=dst, send_sem=send_sem, recv_sem=recv_sem, device_id=(dp, tp, cp), device_id_type=MESH
        )

    def k_copy(b):
        return pltpu.make_async_copy(kc_hbm.at[b], kbuf.at[b % 2], k_sem.at[b % 2])

    def v_copy(b):
        return pltpu.make_async_copy(vc_hbm.at[b], vbuf.at[b % 2], v_sem.at[b % 2])

    def wo_copy(p):
        cols = pl.ds(pl.multiple_of(n_part * width * core + width * p, width), width)
        return pltpu.make_async_copy(wo_hbm.at[:, cols], wo.at[p], wo_sem.at[p])

    def x_copy(j):
        rows = pl.ds(pl.multiple_of(64 * j + 32 * y, 32), 32)
        cols = pl.ds(pl.multiple_of(n_part * width * core + width * z, width), width)
        return pltpu.make_async_copy(x_hbm.at[rows, cols], xs.at[j], xs_sem.at[j])

    k_copy(0).start()
    v_copy(0).start()
    for p in range(n_part):
        wo_copy(p).start()
    for j in range(n_seq):
        x_copy(j).start()

    barrier = pltpu.get_barrier_semaphore()
    for peer in (mate, over):
        pl.semaphore_signal(barrier, inc=1, device_id=(dp, z, peer), device_id_type=MESH)

    @pl.when(z > 0)
    def _():
        pl.semaphore_signal(barrier, inc=1, device_id=(dp, z - 1, c), device_id_type=MESH)

    @pl.when(z < last)
    def _():
        pl.semaphore_signal(barrier, inc=1, device_id=(dp, z + 1, c), device_id_type=MESH)

    @pl.when((z == 0) | (z == last))
    def _():
        pl.semaphore_wait(barrier, 3)

    @pl.when((z > 0) & (z < last))
    def _():
        pl.semaphore_wait(barrier, 4)

    sub16 = lax.broadcasted_iota(jnp.int32, (16, 128), 0) & 1
    even_rows = jnp.where(sub16 == 0, 1.0, 0.0).astype(jnp.bfloat16)
    odd_rows = jnp.where(sub16 == 0, 0.0, 1.0).astype(jnp.bfloat16)
    sub8 = lax.broadcasted_iota(jnp.int32, (8, 256), 0) & 1

    def split_rows(k):
        n = k.shape[0]
        k3 = k.reshape(n // 16, 16, 128)
        return jnp.concatenate(
            [(k3 * even_rows[None]).reshape(n, 128), (k3 * odd_rows[None]).reshape(n, 128)], axis=1
        )

    def split_lanes(v):
        n = v.shape[0]
        lane = lax.broadcasted_iota(jnp.int32, (16, n), 1) & 1
        even = jnp.where(lane == 0, 1.0, 0.0).astype(jnp.bfloat16)
        odd = jnp.where(lane == 0, 0.0, 1.0).astype(jnp.bfloat16)
        vt = v.T.reshape(8, 16, n)
        return jnp.concatenate([(vt * even[None]).reshape(128, n), (vt * odd[None]).reshape(128, n)], axis=0)

    def scores(k):
        return jnp.dot(split_rows(k), qt[...], preferred_element_type=jnp.float32)

    def score_pass(b):
        @pl.when(b + 1 < n_seq)
        def _():
            k_copy(b + 1).start()
            v_copy(b + 1).start()

        q_rows = pl.multiple_of(64 * b, 64)
        for h in range(2):
            blocks = [
                q_ref[h * 2 + g // 2, pl.ds(q_rows + th * 32, 32), (g % 2) * 128 : (g % 2) * 128 + 128]
                for th in range(2)
                for g in range(4)
            ]
            qt[h * 128 : h * 128 + 128, :] = jnp.concatenate(blocks, axis=0).T
        n_rows = 2 * (len_ref[b] - c * (cache_rows // 2))
        k_copy(b).wait()

        def score_tile(t, top):
            sel = pl.ds(pl.multiple_of(t * tile, tile), tile)
            s = scores(kbuf[b % 2, sel, :])
            row = t * tile + lax.broadcasted_iota(jnp.int32, (tile, 256), 0)
            s = jnp.where(row < n_rows, s, MASKED)
            s_buf[sel, :] = s
            return jnp.maximum(top, jnp.max(s.reshape(tile // 8, 8, 256), axis=0))

        top = lax.fori_loop(0, n_tiles, score_tile, jnp.full((8, 256), MASKED, jnp.float32))

        key = lax.broadcasted_iota(jnp.int32, (n_new, 256), 0) // 2
        col = lax.broadcasted_iota(jnp.int32, (n_new, 256), 1)
        token = (col // 128) * 32 + (col % 32)
        token = jnp.where(c == 3, token, -1)
        s_new = jnp.where(key <= token, scores(kn_ref[pl.ds(pl.multiple_of(n_new * b, n_new), n_new), :]), MASKED)
        sn_buf[...] = s_new
        top = jnp.maximum(top, jnp.max(s_new.reshape(n_new // 8, 8, 256), axis=0))
        top0 = jnp.max(jnp.where(sub8 == 0, top, MASKED), axis=0, keepdims=True)
        top1 = jnp.max(jnp.where(sub8 == 0, MASKED, top), axis=0, keepdims=True)
        top_buf[...] = jnp.where(sub8 == 0, top0, top1)

    def weigh_pass(b):
        top = top_buf[...]
        base = jnp.where(top > 0.5 * MASKED, top, 0.0)

        def weigh(s, v):
            n = s.shape[0]
            p = jnp.exp2((s.reshape(n // 8, 8, 256) - base[None]) * EXP2_SCALE)
            total = jnp.sum(p, axis=0)
            out = jnp.dot(split_lanes(v), p.reshape(n, 256).astype(jnp.bfloat16), preferred_element_type=jnp.float32)
            return total, out

        total, out = weigh(sn_buf[...], vn_ref[pl.ds(pl.multiple_of(n_new * b, n_new), n_new), :])
        acc[...] = out
        v_copy(b).wait()

        def weigh_tile(t, total):
            sel = pl.ds(pl.multiple_of(t * tile, tile), tile)
            more, out = weigh(s_buf[sel, :], vbuf[b % 2, sel, :])
            acc[...] += out
            return total + more

        total = lax.fori_loop(0, n_tiles, weigh_tile, total)
        pad = jnp.zeros((6, 256), jnp.float32)
        for h in range(2):
            part[b, h, 0:128, :] = acc[h * 128 : h * 128 + 128, :]
            total_h = jnp.sum(jnp.where(sub8 == h, total, 0.0), axis=0, keepdims=True)
            part[b, h, 128:136, :] = jnp.concatenate([top[h : h + 1], total_h, pad], axis=0)
        a1(b).start()

    def a1(j):
        return send(part.at[j, 1 - core], got1.at[j], a1s.at[j], a1r.at[j], z, mate)

    def a2(j):
        return send(chip.at[j, 1 - y], got2.at[j], a2s.at[j], a2r.at[j], z, over)

    def a3(j, h):
        return send(ob.at[j, h], ob.at[j, h], a3s.at[j], a3r.at[j], z, mate)

    def b_right(j, p):
        return send(prod.at[j, p], from_l.at[j, p], brs.at[j, p], brr.at[j, p], z + 1, c)

    def b_left(j, p):
        return send(prod.at[j, p], from_r.at[j, p], bls.at[j, p], blr.at[j, p], z - 1, c)

    def c_right(j, p):
        return send(full.at[j, c, p], full.at[j, c, p], crs.at[j, p], crr.at[j, p], z + 1, c)

    def c_left(j, p):
        return send(full.at[j, c, p], full.at[j, c, p], cls.at[j, p], clr.at[j, p], z - 1, c)

    def c_over(j, q, p):
        return send(full.at[j, q, p], full.at[j, q, p], cys.at[j, p], cyr.at[j, p], z, over)

    def c_mate(j, q, u, p):
        return send(full.at[j, q, p], full.at[j, q, p], cps.at[j, u, p], cpr.at[j, u, p], z, mate)

    def merge(a, b):
        top = jnp.maximum(a[128:129], b[128:129])
        fa = jnp.exp2((a[128:129] - top) * EXP2_SCALE)
        fb = jnp.exp2((b[128:129] - top) * EXP2_SCALE)
        return a[0:128] * fa + b[0:128] * fb, top, a[129:130] * fa + b[129:130] * fb

    def stage_a1(j):
        a1(j).wait_recv()
        vals, top, total = merge(part[j, core], got1[j])
        for th in range(2):
            sel = slice(128 * th, 128 * th + 128)
            chip[j, th, 0:128] = vals[:, sel]
            chip[j, th, 128:136] = jnp.concatenate([top[:, sel], total[:, sel], jnp.zeros((6, 128), jnp.float32)], axis=0)
        a2(j).start()

    def stage_a2(j):
        a2(j).wait_recv()
        vals, _, total = merge(chip[j, y], got2[j])
        ob[j, core] = (vals / total).T
        a3(j, core).start()

    def stage_a3(j):
        a3(j, 1 - core).wait_recv()

        @pl.when(j == 0)
        def _():
            for p in range(n_part):
                wo_copy(p).wait()

        o = jnp.concatenate([ob[j, h, 32 * g : 32 * g + 32, :] for h in range(2) for g in range(4)], axis=1)
        o = o.astype(jnp.bfloat16)
        for p in range(n_part):
            prod[j, p] = jnp.dot(o, wo[p], preferred_element_type=jnp.float32)

        @pl.when(z == 0)
        def _():
            for p in range(last, 0, -1):
                b_right(j, p).start()

        @pl.when(z == last)
        def _():
            for p in range(last):
                b_left(j, p).start()

    def pass_right(j, p):
        b_right(j, p).wait_recv()
        prod[j, p] = prod[j, p] + from_l[j, p]
        b_right(j, p).start()

    def pass_left(j, p):
        b_left(j, p).wait_recv()
        prod[j, p] = prod[j, p] + from_r[j, p]
        b_left(j, p).start()

    def stage_b1(j):
        @pl.when(z == 1)
        def _():
            pass_right(j, 3)
            pass_right(j, 2)

        @pl.when(z == 2)
        def _():
            pass_left(j, 0)
            pass_left(j, 1)

    def stage_b2(j):
        @pl.when(z == 2)
        def _():
            pass_right(j, 3)

        @pl.when(z == 1)
        def _():
            pass_left(j, 0)

    def stage_c0(j):
        x_copy(j).wait()

        @pl.when(z > 0)
        def _():
            b_right(j, z).wait_recv()
            prod[j, z] = prod[j, z] + from_l[j, z]

        @pl.when(z < last)
        def _():
            b_left(j, z).wait_recv()
            prod[j, z] = prod[j, z] + from_r[j, z]

        full[j, c, z] = prod[j, z] + xs[j].astype(jnp.float32)

        @pl.when(z < last)
        def _():
            c_right(j, z).start()

        @pl.when(z > 0)
        def _():
            c_left(j, z).start()

        c_over(j, c, z).start()
        c_mate(j, c, 0, z).start()

    def stage_c(j, d):
        @pl.when(z - d >= 0)
        def _():
            p = z - d
            c_right(j, p).wait_recv()

            @pl.when(z < last)
            def _():
                c_right(j, p).start()

            c_over(j, c, p).start()
            c_mate(j, c, 0, p).start()

        @pl.when(z + d <= last)
        def _():
            p = z + d
            c_left(j, p).wait_recv()

            @pl.when(z > 0)
            def _():
                c_left(j, p).start()

            c_over(j, c, p).start()
            c_mate(j, c, 0, p).start()

    def stage_over(j):
        for p in range(n_part):
            c_over(j, over, p).wait_recv()
            c_mate(j, over, 1, p).start()

    def out_copy(j):
        return pltpu.make_async_copy(
            stage.at[j], out_hbm.at[pl.ds(pl.multiple_of(64 * j, 64), 64)], out_sem.at[j]
        )

    def stage_out(j):
        for p in range(n_part):
            c_mate(j, mate, 0, p).wait_recv()
            c_mate(j, over_mate, 1, p).wait_recv()
        for q in range(4):
            for p in range(n_part):
                col = width * (n_part * (q % 2) + p)
                stage[j, 32 * (q // 2) : 32 * (q // 2) + 32, col : col + width] = full[j, q, p].astype(jnp.bfloat16)
        out_copy(j).start()

    stages = [
        stage_a1, stage_a2, stage_a3, stage_b1, stage_b2, stage_c0,
        functools.partial(stage_c, d=1), functools.partial(stage_c, d=2), functools.partial(stage_c, d=3),
        stage_over, stage_out,
    ]

    def slot(s, carry):
        b = s // 2

        @pl.when((s % 2 == 0) & (b < n_seq))
        def _():
            score_pass(b)

        @pl.when((s % 2 == 1) & (b < n_seq))
        def _():
            weigh_pass(b)

        for i, stage_fn in enumerate(stages):
            t = s - 2 - i

            @pl.when((t >= 0) & (t % 2 == 0) & (t < 2 * n_seq))
            def _():
                stage_fn(t // 2)

        return carry

    lax.fori_loop(0, 2 * n_seq + len(stages), slot, 0)

    def drain(j, carry):
        a1(j).wait_send()
        a2(j).wait_send()
        a3(j, core).wait_send()
        for p in range(n_part):
            @pl.when(z < p)
            def _():
                b_right(j, p).wait_send()

            @pl.when(z > p)
            def _():
                b_left(j, p).wait_send()

            @pl.when((z >= p) & (z < last))
            def _():
                c_right(j, p).wait_send()

            @pl.when((z <= p) & (z > 0))
            def _():
                c_left(j, p).wait_send()

            c_over(j, c, p).wait_send()
            c_mate(j, c, 0, p).wait_send()
            c_mate(j, over, 1, p).wait_send()
        out_copy(j).wait()
        return carry

    lax.fori_loop(0, n_seq, drain, 0)


def attend_and_project(prefix_len, q3, kn, vn, kc, vc, x2, w_o):
    rows, d_model = x2.shape
    n_seq, cache_rows, _ = kc.shape
    n_part = 4
    width = d_model // (2 * n_part)
    new_rows = kn.shape[0] // n_seq
    tile = min(2048, cache_rows)
    any_spec = pl.BlockSpec(memory_space=pl.ANY)
    vmem = pl.BlockSpec(memory_space=pltpu.VMEM)
    f32, bf16 = jnp.float32, jnp.bfloat16
    sems = pltpu.SemaphoreType.DMA
    piece = (32, width)
    return pl.pallas_call(
        functools.partial(block_kernel, tile=tile),
        out_shape=jax.ShapeDtypeStruct((rows, d_model), bf16),
        in_specs=[pl.BlockSpec(memory_space=pltpu.SMEM), vmem, vmem, vmem, any_spec, any_spec, any_spec, any_spec],
        out_specs=any_spec,
        scratch_shapes=[
            pltpu.VMEM((2, cache_rows, 128), bf16),
            pltpu.VMEM((2, cache_rows, 128), bf16),
            pltpu.VMEM((256, 256), bf16),
            pltpu.VMEM((cache_rows, 256), f32),
            pltpu.VMEM((new_rows, 256), f32),
            pltpu.VMEM((256, 256), f32),
            pltpu.VMEM((8, 256), f32),
            pltpu.VMEM((n_part, w_o.shape[0], width), bf16),
            pltpu.VMEM((n_seq, *piece), bf16),
            pltpu.VMEM((n_seq, 2, 136, 256), f32),
            pltpu.VMEM((n_seq, 136, 256), f32),
            pltpu.VMEM((n_seq, 2, 136, 128), f32),
            pltpu.VMEM((n_seq, 136, 128), f32),
            pltpu.VMEM((n_seq, 2, 128, 128), f32),
            pltpu.VMEM((n_seq, n_part, *piece), f32),
            pltpu.VMEM((n_seq, n_part, *piece), f32),
            pltpu.VMEM((n_seq, n_part, *piece), f32),
            pltpu.VMEM((n_seq, 4, n_part, *piece), f32),
            pltpu.VMEM((n_seq, 64, d_model), bf16),
            sems((2,)),
            sems((2,)),
            sems((n_part,)),
            sems((n_seq,)),
            sems((n_seq,)),
            *[sems((n_seq,))] * 6,
            *[sems((n_seq, n_part))] * 10,
            sems((n_seq, 2, n_part)),
            sems((n_seq, 2, n_part)),
        ],
        compiler_params=pltpu.CompilerParams(
            collective_id=0, has_side_effects=True, vmem_limit_bytes=63 * 1024 * 1024
        ),
        cost_estimate=pl.CostEstimate(
            flops=4 * n_seq * cache_rows * 256 * 256, bytes_accessed=60 << 20, transcendentals=n_seq * cache_rows * 256
        ),
        name="attend_and_project",
    )(prefix_len, q3, kn, vn, kc, vc, x2, w_o)


def solution(mesh):
    def per_device(hidden, prefix_len, k_cache, v_cache, attn_norm, w_q, w_k, w_v, w_o, q_norm, k_norm):
        n_seq, n_new, d_model = hidden.shape
        x2 = hidden.reshape(n_seq * n_new, d_model)
        q3, k_rows, v_rows = project(prefix_len, x2, attn_norm, w_q, w_k, w_v, q_norm, k_norm)
        out = attend_and_project(
            prefix_len, q3, k_rows, v_rows,
            k_cache.reshape(n_seq, -1, HEAD_DIM), v_cache.reshape(n_seq, -1, HEAD_DIM), x2, w_o,
        )
        new_shape = (n_seq, n_new, 2, HEAD_DIM)
        return out.reshape(hidden.shape), k_rows.reshape(new_shape), v_rows.reshape(new_shape)

    cache_spec = P("dp", "cp", "tp", None)
    arg_specs = (P("dp", None, None), P("dp"), cache_spec, cache_spec, P(None), P(None, "tp"), P(None, "tp"), P(None, "tp"), P("tp", None), P(None), P(None))
    out_specs = (P("dp", None, None), P("dp", None, "tp", None), P("dp", None, "tp", None))
    return jax.shard_map(per_device, mesh=mesh, in_specs=arg_specs, out_specs=out_specs, check_vma=False)
```

time: 158 us -> 130 us (0.82); the launches traced: 156 us -> 130 us
  Pallas kernels: 151 us -> 125 us
    pallas_call x2 -> x1, Pallas kernels: 132 us -> 106 us  [attend_and_project(): pl.pallas_call(functools.partial(block_kernel, tile=tile), out_shape=jax....]
where the time goes in v3:
time: 130 us
  Pallas kernels  125 us (96%)
  local copies, waits for them, and re-layouts  4.7 us (4%)
    pallas_call x1, Pallas kernels, attend_and_project(): pl.pallas_call(functools.partial(block_kernel, tile=tile), out_shape=jax....  106 us
    pallas_call x1, Pallas kernels, project(): pl.pallas_call(project_kernel, out_shape=(jax.ShapeDtypeStruct((n_q, rows...  18.6 us
    unnamed x1, local copies, waits for them, and re-layouts  4.7 us

profile of v3, /device:TPU:1, one launch (start us, length us, event | category | flops | bytes accessed | tf_op | source)
XLA Modules:
  0.0 130.1 jit_solution(7198693850092614145)
XLA Ops:
  0.6 18.6 %project.1 = (bf16[4,512,256]{2,1,0:T(8,128)(2,1)}, bf16[1024,128]{1,0:T(8,128)(2,1)}, bf16[1024,128]{1,0:T(8,128)(2,1)}) custom-call(s32[8]{0:T(128)} %len_ref.3, bf16[512,4096]{1,0:T(8,128)(2,1)} %bitcast.9, bf16[4096]{0:T(1024)(128)(2,1)} %gain.1, bf16[4096,1024]{1,0:T(8,128)(2,1)} %wq_hbm.1, bf16[4096,256]{1,0:T(8,128)(2,1)} %wk_hbm.1, ...), custom_call_target="tpu_custom_call" | custom-call | flops 6442450944 | bytes 20971520 | tf_op jit(solution)/shard_map/project/pallas_call | solution.py:108
  19.3 106.1 %attend_and_project.1 = bf16[512,4096]{1,0:T(8,128)(2,1)} custom-call(s32[8]{0:T(128)} %len_ref.3, bf16[4,512,256]{2,1,0:T(8,128)(2,1)} %get-tuple-element.6.q_ref, bf16[1024,128]{1,0:T(8,128)(2,1)} %get-tuple-element.7.kn_ref, bf16[1024,128]{1,0:T(8,128)(2,1)} %get-tuple-element.8.vn_ref, bf16[8,8192,128]{2,1,0:T(8,128)(2,1)} %bitcast.7, ...), custom_call_target="tpu_custom_call" | custom-call | flops 17179869184 | bytes 62914560 | tf_op jit(solution)/shard_map/attend_and_project/pallas_call | solution.py:532
  125.4 4.7 %copy.16 = bf16[8,64,4096]{2,1,0:T(8,128)(2,1)} copy(bf16[8,64,4096]{2,1,0:T(8,128)(2,1)} %bitcast.6) | data formatting | bytes 8388608

commit v4 on v3

--- a/solution.py
+++ b/solution.py
@@ -133,10 +133,10 @@
 
 
 def block_kernel(
-    len_ref, q_ref, kn_ref, vn_ref, kc_hbm, vc_hbm, x_hbm, wo_hbm, out_hbm,
-    kbuf, vbuf, qt, s_buf, sn_buf, acc, top_buf,
-    wo, xs, part, got1, chip, got2, ob, prod, from_l, from_r, full, stage,
-    k_sem, v_sem, wo_sem, xs_sem, out_sem, a1s, a1r, a2s, a2r, a3s, a3r,
+    len_ref, q_ref, kn_ref, vn_ref, kc_hbm, vc_hbm, x_hbm, wo_hbm, out_ref,
+    kbuf, vbuf, qt, s_buf, sn_buf, acc, top_buf, run_top, run_sum,
+    wo, xs, part, got1, chip, got2, ob, prod, from_l, from_r, full,
+    k_sem, v_sem, wo_sem, xs_sem, a1s, a1r, a2s, a2r, a3s, a3r,
     brs, brr, bls, blr, crs, crr, cls, clr, cys, cyr, cps, cpr, *, tile,
 ):
     dp, z, c = lax.axis_index("dp"), lax.axis_index("tp"), lax.axis_index("cp")
@@ -220,12 +220,16 @@
     def scores(k):
         return jnp.dot(split_rows(k), qt[...], preferred_element_type=jnp.float32)
 
-    def score_pass(b):
+    def fetch(b):
         @pl.when(b + 1 < n_seq)
         def _():
             k_copy(b + 1).start()
-            v_copy(b + 1).start()
-
+
+        @pl.when((b > 0) & (b < n_seq))
+        def _():
+            v_copy(b).start()
+
+    def score_start(b):
         q_rows = pl.multiple_of(64 * b, 64)
         for h in range(2):
             blocks = [
@@ -234,58 +238,101 @@
                 for g in range(4)
             ]
             qt[h * 128 : h * 128 + 128, :] = jnp.concatenate(blocks, axis=0).T
-        n_rows = 2 * (len_ref[b] - c * (cache_rows // 2))
+        run_top[...] = jnp.full((8, 256), MASKED, jnp.float32)
         k_copy(b).wait()
 
-        def score_tile(t, top):
-            sel = pl.ds(pl.multiple_of(t * tile, tile), tile)
-            s = scores(kbuf[b % 2, sel, :])
-            row = t * tile + lax.broadcasted_iota(jnp.int32, (tile, 256), 0)
-            s = jnp.where(row < n_rows, s, MASKED)
-            s_buf[sel, :] = s
-            return jnp.maximum(top, jnp.max(s.reshape(tile // 8, 8, 256), axis=0))
-
-        top = lax.fori_loop(0, n_tiles, score_tile, jnp.full((8, 256), MASKED, jnp.float32))
-
+    def score_tile(b, t):
+        sel = pl.ds(pl.multiple_of(t * tile, tile), tile)
+        n_rows = 2 * (len_ref[b] - c * (cache_rows // 2)) - t * tile
+        s = scores(kbuf[b % 2, sel, :])
+        s = jnp.where(lax.broadcasted_iota(jnp.int32, (tile, 256), 0) < n_rows, s, MASKED)
+        s_buf[sel, :] = s
+        run_top[...] = jnp.maximum(run_top[...], jnp.max(s.reshape(tile // 8, 8, 256), axis=0))
+
+    def score_end(b):
         key = lax.broadcasted_iota(jnp.int32, (n_new, 256), 0) // 2
         col = lax.broadcasted_iota(jnp.int32, (n_new, 256), 1)
         token = (col // 128) * 32 + (col % 32)
         token = jnp.where(c == 3, token, -1)
         s_new = jnp.where(key <= token, scores(kn_ref[pl.ds(pl.multiple_of(n_new * b, n_new), n_new), :]), MASKED)
         sn_buf[...] = s_new
-        top = jnp.maximum(top, jnp.max(s_new.reshape(n_new // 8, 8, 256), axis=0))
+        top = jnp.maximum(run_top[...], jnp.max(s_new.reshape(n_new // 8, 8, 256), axis=0))
         top0 = jnp.max(jnp.where(sub8 == 0, top, MASKED), axis=0, keepdims=True)
         top1 = jnp.max(jnp.where(sub8 == 0, MASKED, top), axis=0, keepdims=True)
         top_buf[...] = jnp.where(sub8 == 0, top0, top1)
 
-    def weigh_pass(b):
+    def weigh(s, v):
         top = top_buf[...]
         base = jnp.where(top > 0.5 * MASKED, top, 0.0)
-
-        def weigh(s, v):
-            n = s.shape[0]
-            p = jnp.exp2((s.reshape(n // 8, 8, 256) - base[None]) * EXP2_SCALE)
-            total = jnp.sum(p, axis=0)
-            out = jnp.dot(split_lanes(v), p.reshape(n, 256).astype(jnp.bfloat16), preferred_element_type=jnp.float32)
-            return total, out
-
-        total, out = weigh(sn_buf[...], vn_ref[pl.ds(pl.multiple_of(n_new * b, n_new), n_new), :])
-        acc[...] = out
+        n = s.shape[0]
+        p = jnp.exp2((s.reshape(n // 8, 8, 256) - base[None]) * EXP2_SCALE)
+        out = jnp.dot(split_lanes(v), p.reshape(n, 256).astype(jnp.bfloat16), preferred_element_type=jnp.float32)
+        return jnp.sum(p, axis=0), out
+
+    def weigh_start(b):
+        run_sum[...], acc[...] = weigh(sn_buf[...], vn_ref[pl.ds(pl.multiple_of(n_new * b, n_new), n_new), :])
         v_copy(b).wait()
 
-        def weigh_tile(t, total):
-            sel = pl.ds(pl.multiple_of(t * tile, tile), tile)
-            more, out = weigh(s_buf[sel, :], vbuf[b % 2, sel, :])
-            acc[...] += out
-            return total + more
-
-        total = lax.fori_loop(0, n_tiles, weigh_tile, total)
+    def weigh_tile(b, t):
+        sel = pl.ds(pl.multiple_of(t * tile, tile), tile)
+        more, out = weigh(s_buf[sel, :], vbuf[b % 2, sel, :])
+        acc[...] += out
+        run_sum[...] += more
+
+    def weigh_end(b):
+        total = run_sum[...]
         pad = jnp.zeros((6, 256), jnp.float32)
         for h in range(2):
             part[b, h, 0:128, :] = acc[h * 128 : h * 128 + 128, :]
             total_h = jnp.sum(jnp.where(sub8 == h, total, 0.0), axis=0, keepdims=True)
-            part[b, h, 128:136, :] = jnp.concatenate([top[h : h + 1], total_h, pad], axis=0)
+            part[b, h, 128:136, :] = jnp.concatenate([top_buf[h : h + 1, :], total_h, pad], axis=0)
         a1(b).start()
+
+    def attend(s):
+        b, first = s // 2, s % 2 == 0
+
+        @pl.when(first)
+        def _():
+            fetch(b)
+
+        @pl.when(first & (b < n_seq))
+        def _():
+            score_start(b)
+
+        @pl.when(first & (b > 0))
+        def _():
+            weigh_start(b - 1)
+
+        def tiles(body):
+            def one(i, carry):
+                body((s % 2) * (n_tiles // 2) + i)
+                return carry
+
+            lax.fori_loop(0, n_tiles // 2, one, 0)
+
+        @pl.when(b == 0)
+        def _():
+            tiles(lambda t: score_tile(b, t))
+
+        @pl.when((b > 0) & (b < n_seq))
+        def _():
+            def both(t):
+                weigh_tile(b - 1, t)
+                score_tile(b, t)
+
+            tiles(both)
+
+        @pl.when(b == n_seq)
+        def _():
+            tiles(lambda t: weigh_tile(b - 1, t))
+
+        @pl.when((s % 2 == 1) & (b > 0))
+        def _():
+            weigh_end(b - 1)
+
+        @pl.when((s % 2 == 1) & (b < n_seq))
+        def _():
+            score_end(b)
 
     def a1(j):
         return send(part.at[j, 1 - core], got1.at[j], a1s.at[j], a1r.at[j], z, mate)
@@ -444,11 +491,6 @@
             c_over(j, over, p).wait_recv()
             c_mate(j, over, 1, p).start()
 
-    def out_copy(j):
-        return pltpu.make_async_copy(
-            stage.at[j], out_hbm.at[pl.ds(pl.multiple_of(64 * j, 64), 64)], out_sem.at[j]
-        )
-
     def stage_out(j):
         for p in range(n_part):
             c_mate(j, mate, 0, p).wait_recv()
@@ -456,28 +498,25 @@
         for q in range(4):
             for p in range(n_part):
                 col = width * (n_part * (q % 2) + p)
-                stage[j, 32 * (q // 2) : 32 * (q // 2) + 32, col : col + width] = full[j, q, p].astype(jnp.bfloat16)
-        out_copy(j).start()
+                rows = pl.ds(pl.multiple_of(64 * j + 32 * (q // 2), 32), 32)
+                out_ref[rows, col : col + width] = full[j, q, p].astype(jnp.bfloat16)
 
     stages = [
-        stage_a1, stage_a2, stage_a3, stage_b1, stage_b2, stage_c0,
-        functools.partial(stage_c, d=1), functools.partial(stage_c, d=2), functools.partial(stage_c, d=3),
-        stage_over, stage_out,
+        (stage_a1, 1), (stage_a2, 2), (stage_a3, 1), (stage_b1, 3), (stage_b2, 2), (stage_c0, 2),
+        (functools.partial(stage_c, d=1), 2), (functools.partial(stage_c, d=2), 3), (functools.partial(stage_c, d=3), 2),
+        (stage_over, 5), (stage_out, 5),
     ]
+    n_slots = 2 * n_seq + 2 + sum(lag for _, lag in stages)
 
     def slot(s, carry):
-        b = s // 2
-
-        @pl.when((s % 2 == 0) & (b < n_seq))
-        def _():
-            score_pass(b)
-
-        @pl.when((s % 2 == 1) & (b < n_seq))
-        def _():
-            weigh_pass(b)
-
-        for i, stage_fn in enumerate(stages):
-            t = s - 2 - i
+        @pl.when(s < 2 * n_seq + 2)
+        def _():
+            attend(s)
+
+        after = 3 + sum(lag for _, lag in stages)
+        for stage_fn, lag in reversed(stages):
+            t = s - after
+            after -= lag
 
             @pl.when((t >= 0) & (t % 2 == 0) & (t < 2 * n_seq))
             def _():
@@ -485,7 +524,7 @@
 
         return carry
 
-    lax.fori_loop(0, 2 * n_seq + len(stages), slot, 0)
+    lax.fori_loop(0, n_slots, slot, 0)
 
     def drain(j, carry):
         a1(j).wait_send()
@@ -511,7 +550,6 @@
             c_over(j, c, p).wait_send()
             c_mate(j, c, 0, p).wait_send()
             c_mate(j, over, 1, p).wait_send()
-        out_copy(j).wait()
         return carry
 
     lax.fori_loop(0, n_seq, drain, 0)
@@ -531,9 +569,9 @@
     piece = (32, width)
     return pl.pallas_call(
         functools.partial(block_kernel, tile=tile),
-        out_shape=jax.ShapeDtypeStruct((rows, d_model), bf16),
+        out_shape=pltpu.VMEM((rows, d_model), bf16),
         in_specs=[pl.BlockSpec(memory_space=pltpu.SMEM), vmem, vmem, vmem, any_spec, any_spec, any_spec, any_spec],
-        out_specs=any_spec,
+        out_specs=vmem,
         scratch_shapes=[
             pltpu.VMEM((2, cache_rows, 128), bf16),
             pltpu.VMEM((2, cache_rows, 128), bf16),
@@ -541,6 +579,8 @@
             pltpu.VMEM((cache_rows, 256), f32),
             pltpu.VMEM((new_rows, 256), f32),
             pltpu.VMEM((256, 256), f32),
+            pltpu.VMEM((8, 256), f32),
+            pltpu.VMEM((8, 256), f32),
             pltpu.VMEM((8, 256), f32),
             pltpu.VMEM((n_part, w_o.shape[0], width), bf16),
             pltpu.VMEM((n_seq, *piece), bf16),
@@ -553,11 +593,9 @@
             pltpu.VMEM((n_seq, n_part, *piece), f32),
             pltpu.VMEM((n_seq, n_part, *piece), f32),
             pltpu.VMEM((n_seq, 4, n_part, *piece), f32),
-            pltpu.VMEM((n_seq, 64, d_model), bf16),
             sems((2,)),
             sems((2,)),
             sems((n_part,)),
-            sems((n_seq,)),
             sems((n_seq,)),
             *[sems((n_seq,))] * 6,
             *[sems((n_seq, n_part))] * 10,
@@ -565,7 +603,7 @@
             sems((n_seq, 2, n_part)),
         ],
         compiler_params=pltpu.CompilerParams(
-            collective_id=0, has_side_effects=True, vmem_limit_bytes=63 * 1024 * 1024
+            collective_id=0, has_side_effects=True, vmem_limit_bytes=57 * 1024 * 1024
         ),
         cost_estimate=pl.CostEstimate(
             flops=4 * n_seq * cache_rows * 256 * 256, bytes_accessed=60 << 20, transcendentals=n_seq * cache_rows * 256

time: 130 us -> 122 us (0.938)
  Pallas kernels: 125 us -> 119 us
  local copies, waits for them, and re-layouts: 4.7 us -> 2.02 us
    pallas_call x1, Pallas kernels: 106 us -> 99.9 us  [attend_and_project(): pl.pallas_call(functools.partial(block_kernel, tile=tile), out_shape=pltp...]
    unnamed x1, local copies, waits for them, and re-layouts: 4.7 us -> 2.02 us
where the time goes in v4:
time: 122 us; the launch traced here: 121 us
  Pallas kernels  119 us (98%)
  local copies, waits for them, and re-layouts  2.02 us (2%)
    pallas_call x1, Pallas kernels, attend_and_project(): pl.pallas_call(functools.partial(block_kernel, tile=tile), out_shape=pltp...  99.9 us
    pallas_call x1, Pallas kernels, project(): pl.pallas_call(project_kernel, out_shape=(jax.ShapeDtypeStruct((n_q, rows...  18.6 us

profile of v4, /device:TPU:1, one launch (start us, length us, event | category | flops | bytes accessed | tf_op | source)
XLA Modules:
  0.0 121.2 jit_solution(9228530895639351165)
XLA Ops:
  0.6 18.6 %project.1 = (bf16[4,512,256]{2,1,0:T(8,128)(2,1)}, bf16[1024,128]{1,0:T(8,128)(2,1)}, bf16[1024,128]{1,0:T(8,128)(2,1)}) custom-call(s32[8]{0:T(128)} %len_ref.3, bf16[512,4096]{1,0:T(8,128)(2,1)} %bitcast.9, bf16[4096]{0:T(1024)(128)(2,1)} %gain.1, bf16[4096,1024]{1,0:T(8,128)(2,1)} %wq_hbm.1, bf16[4096,256]{1,0:T(8,128)(2,1)} %wk_hbm.1, ...), custom_call_target="tpu_custom_call" | custom-call | flops 6442450944 | bytes 20971520 | tf_op jit(solution)/shard_map/project/pallas_call | solution.py:108
  19.3 99.9 %attend_and_project.1 = bf16[512,4096]{1,0:T(8,128)(2,1)S(1)} custom-call(s32[8]{0:T(128)} %len_ref.3, bf16[4,512,256]{2,1,0:T(8,128)(2,1)} %get-tuple-element.6.q_ref, bf16[1024,128]{1,0:T(8,128)(2,1)} %get-tuple-element.7.kn_ref, bf16[1024,128]{1,0:T(8,128)(2,1)} %get-tuple-element.8.vn_ref, bf16[8,8192,128]{2,1,0:T(8,128)(2,1)} %bitcast.7, ...), custom_call_target="tpu_custom_call" | custom-call | flops 17179869184 | bytes 62914560 | tf_op jit(solution)/shard_map/attend_and_project/pallas_call | solution.py:570
  119.2 2.0 %copy.16 = bf16[8,64,4096]{2,1,0:T(8,128)(2,1)} copy(bf16[8,64,4096]{2,1,0:T(8,128)(2,1)S(1)} %bitcast.6) | data formatting | bytes 8388608

commit v5 on v4

--- a/solution.py
+++ b/solution.py
@@ -14,129 +14,12 @@
 MESH = pl.DeviceIdType.MESH
 
 
-def project_kernel(
-    len_ref, x_hbm, gain, wq_hbm, wk_hbm, wv_hbm, q_gain, k_gain, freq,
-    q_out, k_out, v_out, x_buf, h_buf, w_buf, cos_t, sin_t, turn, x_sem, w_sem,
-):
-    rows, d_model = x_buf.shape
-    n_q = wq_hbm.shape[1] // 256
-    n_seq = len_ref.shape[0]
-    n_new = rows // n_seq
-    piece = rows // 4
-    x_copies = [
-        pltpu.make_async_copy(x_hbm.at[pl.ds(piece * i, piece)], x_buf.at[pl.ds(piece * i, piece)], x_sem.at[i])
-        for i in range(4)
-    ]
-    for copy in x_copies:
-        copy.start()
-    w_copies = [
-        pltpu.make_async_copy(wq_hbm.at[:, pl.ds(256 * i, 256)], w_buf.at[i], w_sem.at[i]) for i in range(n_q)
-    ]
-    w_copies.append(pltpu.make_async_copy(wk_hbm, w_buf.at[n_q], w_sem.at[n_q]))
-    w_copies.append(pltpu.make_async_copy(wv_hbm, w_buf.at[n_q + 1], w_sem.at[n_q + 1]))
-
-    lane = lax.broadcasted_iota(jnp.int32, (n_new, 128), 1)
-    token = lax.broadcasted_iota(jnp.int32, (n_new, 128), 0)
-
-    def rope_rows(b, carry):
-        angle = (token + len_ref[b]).astype(jnp.float32) * freq[...]
-        sel = pl.ds(pl.multiple_of(b * n_new, n_new), n_new)
-        cos_t[sel, :] = jnp.cos(angle)
-        sin = jnp.sin(angle)
-        sin_t[sel, :] = jnp.where(lane < 64, -sin, sin)
-        return carry
-
-    lax.fori_loop(0, n_seq, rope_rows, 0)
-    x_gain = gain[...].astype(jnp.float32).reshape(1, d_model)
-
-    def norm_rows(i, carry):
-        sel = pl.ds(pl.multiple_of(i * 32, 32), 32)
-        x = x_buf[sel, :].astype(jnp.float32)
-        mean_sq = jnp.mean(x * x, axis=-1, keepdims=True)
-        h_buf[sel, :] = (x * lax.rsqrt(mean_sq + 1e-6) * x_gain).astype(jnp.bfloat16)
-        return carry
-
-    for i in range(4):
-        x_copies[i].wait()
-        if i == 0:
-            for copy in w_copies:
-                copy.start()
-    lax.fori_loop(0, rows // 32, norm_rows, 0)
-    q_gain_row = q_gain[...].astype(jnp.float32).reshape(1, 128)
-    k_gain_row = k_gain[...].astype(jnp.float32).reshape(1, 128)
-
-    def one_tile(i, carry):
-        pltpu.make_async_copy(w_buf.at[i], w_buf.at[i], w_sem.at[i]).wait()
-        lin = jnp.dot(h_buf[...], w_buf[i], preferred_element_type=jnp.float32).astype(jnp.bfloat16)
-        lin = lin.astype(jnp.float32)
-        head_gain = jnp.where(i < n_q, q_gain_row, k_gain_row)
-        for u in range(2):
-            raw = lin[:, 128 * u : 128 * u + 128]
-            mean_sq = jnp.mean(raw * raw, axis=-1, keepdims=True)
-            t = raw * lax.rsqrt(mean_sq + 1e-6) * head_gain
-            t = t * cos_t[...] + pltpu.roll(t, 64, 1) * sin_t[...]
-
-            @pl.when(i < n_q)
-            def _():
-                q_out[i, :, 128 * u : 128 * u + 128] = t.astype(jnp.bfloat16)
-
-            @pl.when(i >= n_q)
-            def _():
-                turn[pl.ds(u, rows, stride=2), :] = jnp.where(i == n_q, t, raw)
-
-        @pl.when(i == n_q)
-        def _():
-            k_out[...] = turn[...].astype(jnp.bfloat16)
-
-        @pl.when(i == n_q + 1)
-        def _():
-            v_out[...] = turn[...].astype(jnp.bfloat16)
-
-        return carry
-
-    lax.fori_loop(0, n_q + 2, one_tile, 0)
-
-
-def project(prefix_len, x2, gain, w_q, w_k, w_v, q_gain, k_gain):
-    rows, d_model = x2.shape
-    n_q = w_q.shape[1] // 256
-    half_dim = HEAD_DIM // 2
-    freq = 1.0 / (1000000.0 ** (np.arange(half_dim, dtype=np.float64) * 2.0 / HEAD_DIM))
-    freq = jnp.asarray(np.concatenate([freq, freq])[None], jnp.float32)
-    any_spec = pl.BlockSpec(memory_space=pl.ANY)
-    vmem = pl.BlockSpec(memory_space=pltpu.VMEM)
-    return pl.pallas_call(
-        project_kernel,
-        out_shape=(
-            jax.ShapeDtypeStruct((n_q, rows, 256), jnp.bfloat16),
-            jax.ShapeDtypeStruct((2 * rows, 128), jnp.bfloat16),
-            jax.ShapeDtypeStruct((2 * rows, 128), jnp.bfloat16),
-        ),
-        in_specs=[pl.BlockSpec(memory_space=pltpu.SMEM), any_spec, vmem, any_spec, any_spec, any_spec, vmem, vmem, vmem],
-        out_specs=(vmem, vmem, vmem),
-        scratch_shapes=[
-            pltpu.VMEM((rows, d_model), jnp.bfloat16),
-            pltpu.VMEM((rows, d_model), jnp.bfloat16),
-            pltpu.VMEM((n_q + 2, d_model, 256), jnp.bfloat16),
-            pltpu.VMEM((rows, 128), jnp.float32),
-            pltpu.VMEM((rows, 128), jnp.float32),
-            pltpu.VMEM((2 * rows, 128), jnp.float32),
-            pltpu.SemaphoreType.DMA((4,)),
-            pltpu.SemaphoreType.DMA((n_q + 2,)),
-        ],
-        compiler_params=pltpu.CompilerParams(vmem_limit_bytes=56 * 1024 * 1024),
-        cost_estimate=pl.CostEstimate(
-            flops=2 * rows * d_model * 256 * (n_q + 2), bytes_accessed=20 << 20, transcendentals=0
-        ),
-        name="project",
-    )(prefix_len, x2, gain, w_q, w_k, w_v, q_gain, k_gain, freq)
-
-
 def block_kernel(
-    len_ref, q_ref, kn_ref, vn_ref, kc_hbm, vc_hbm, x_hbm, wo_hbm, out_ref,
-    kbuf, vbuf, qt, s_buf, sn_buf, acc, top_buf, run_top, run_sum,
+    len_ref, gain, q_gain, k_gain, freq, x_hbm, wq_hbm, wk_hbm, wv_hbm, kc_hbm, vc_hbm, wo_hbm,
+    out_ref, kn_ref, vn_ref,
+    q_ref, w_buf, cos_t, sin_t, turn, kbuf, vbuf, qt, s_buf, sn_buf, acc, top_buf, run_top, run_sum,
     wo, xs, part, got1, chip, got2, ob, prod, from_l, from_r, full,
-    k_sem, v_sem, wo_sem, xs_sem, a1s, a1r, a2s, a2r, a3s, a3r,
+    x_sem, w_sem, k_sem, v_sem, wo_sem, xs_sem, a1s, a1r, a2s, a2r, a3s, a3r,
     brs, brr, bls, blr, crs, crr, cls, clr, cys, cyr, cps, cpr, *, tile,
 ):
     dp, z, c = lax.axis_index("dp"), lax.axis_index("tp"), lax.axis_index("cp")
@@ -148,7 +31,11 @@
     last = n_part - 1
     cache_rows = kbuf.shape[1]
     n_new = kn_ref.shape[0] // n_seq
+    n_tok = n_new // 2
     n_tiles = cache_rows // tile
+    rows, d_model = out_ref.shape
+    half_rows = rows // 2
+    n_q = wq_hbm.shape[1] // 256
 
     def send(src, dst, send_sem, recv_sem, tp, cp):
         return pltpu.make_async_remote_copy(
@@ -170,24 +57,103 @@
         cols = pl.ds(pl.multiple_of(n_part * width * core + width * z, width), width)
         return pltpu.make_async_copy(x_hbm.at[rows, cols], xs.at[j], xs_sem.at[j])
 
+    def in_copy(half):
+        sel = pl.ds(half_rows * half, half_rows)
+        return pltpu.make_async_copy(x_hbm.at[sel], out_ref.at[sel], x_sem.at[half])
+
+    w_copies = [
+        pltpu.make_async_copy(wq_hbm.at[:, pl.ds(256 * i, 256)], w_buf.at[i], w_sem.at[i]) for i in range(n_q)
+    ]
+    w_copies.append(pltpu.make_async_copy(wk_hbm, w_buf.at[n_q], w_sem.at[n_q]))
+    w_copies.append(pltpu.make_async_copy(wv_hbm, w_buf.at[n_q + 1], w_sem.at[n_q + 1]))
+    in_copy(0).start()
+
+    barrier = pltpu.get_barrier_semaphore()
+    for peer in (mate, over):
+        pl.semaphore_signal(barrier, inc=1, device_id=(dp, z, peer), device_id_type=MESH)
+
+    @pl.when(z > 0)
+    def _():
+        pl.semaphore_signal(barrier, inc=1, device_id=(dp, z - 1, c), device_id_type=MESH)
+
+    @pl.when(z < last)
+    def _():
+        pl.semaphore_signal(barrier, inc=1, device_id=(dp, z + 1, c), device_id_type=MESH)
+
+    rope_lane = lax.broadcasted_iota(jnp.int32, (n_tok, 128), 1)
+    rope_token = lax.broadcasted_iota(jnp.int32, (n_tok, 128), 0)
+
+    def rope_rows(b, carry):
+        angle = (rope_token + len_ref[b]).astype(jnp.float32) * freq[...]
+        sel = pl.ds(pl.multiple_of(b * (n_tok), n_tok), n_tok)
+        cos_t[sel, :] = jnp.cos(angle)
+        sin = jnp.sin(angle)
+        sin_t[sel, :] = jnp.where(rope_lane < 64, -sin, sin)
+        return carry
+
+    lax.fori_loop(0, n_seq, rope_rows, 0)
+    x_gain = gain[...].astype(jnp.float32).reshape(1, d_model)
+
+    def norm_half(half):
+        def norm_rows(i, carry):
+            sel = pl.ds(pl.multiple_of(half * half_rows + i * 32, 32), 32)
+            x = out_ref[sel, :].astype(jnp.float32)
+            mean_sq = jnp.mean(x * x, axis=-1, keepdims=True)
+            out_ref[sel, :] = (x * lax.rsqrt(mean_sq + 1e-6) * x_gain).astype(jnp.bfloat16)
+            return carry
+
+        lax.fori_loop(0, half_rows // 32, norm_rows, 0)
+
+    q_gain_row = q_gain[...].astype(jnp.float32).reshape(1, 128)
+    k_gain_row = k_gain[...].astype(jnp.float32).reshape(1, 128)
+
+    def project_tile(i, half):
+        sel = slice(half * half_rows, (half + 1) * half_rows)
+        lin = jnp.dot(out_ref[sel, :], w_buf[i], preferred_element_type=jnp.float32).astype(jnp.bfloat16)
+        lin = lin.astype(jnp.float32)
+        head_gain = jnp.where(i < n_q, q_gain_row, k_gain_row)
+        for u in range(2):
+            raw = lin[:, 128 * u : 128 * u + 128]
+            mean_sq = jnp.mean(raw * raw, axis=-1, keepdims=True)
+            t = raw * lax.rsqrt(mean_sq + 1e-6) * head_gain
+            t = t * cos_t[sel, :] + pltpu.roll(t, 64, 1) * sin_t[sel, :]
+
+            @pl.when(i < n_q)
+            def _():
+                q_ref[i, sel, 128 * u : 128 * u + 128] = t.astype(jnp.bfloat16)
+
+            @pl.when(i >= n_q)
+            def _():
+                turn[pl.ds(u, half_rows, stride=2), :] = jnp.where(i == n_q, t, raw)
+
+        new_rows = slice(half * rows, (half + 1) * rows)
+
+        @pl.when(i == n_q)
+        def _():
+            kn_ref[new_rows, :] = turn[...].astype(jnp.bfloat16)
+
+        @pl.when(i == n_q + 1)
+        def _():
+            vn_ref[new_rows, :] = turn[...].astype(jnp.bfloat16)
+
+    in_copy(0).wait()
+    for copy in w_copies:
+        copy.start()
+    norm_half(0)
     k_copy(0).start()
+    in_copy(1).start()
+
+    def first_tile(i, carry):
+        pltpu.make_async_copy(w_buf.at[i], w_buf.at[i], w_sem.at[i]).wait()
+        project_tile(i, 0)
+        return carry
+
+    lax.fori_loop(0, n_q + 2, first_tile, 0)
     v_copy(0).start()
     for p in range(n_part):
         wo_copy(p).start()
     for j in range(n_seq):
         x_copy(j).start()
-
-    barrier = pltpu.get_barrier_semaphore()
-    for peer in (mate, over):
-        pl.semaphore_signal(barrier, inc=1, device_id=(dp, z, peer), device_id_type=MESH)
-
-    @pl.when(z > 0)
-    def _():
-        pl.semaphore_signal(barrier, inc=1, device_id=(dp, z - 1, c), device_id_type=MESH)
-
-    @pl.when(z < last)
-    def _():
-        pl.semaphore_signal(barrier, inc=1, device_id=(dp, z + 1, c), device_id_type=MESH)
 
     @pl.when((z == 0) | (z == last))
     def _():
@@ -509,6 +475,15 @@
     n_slots = 2 * n_seq + 2 + sum(lag for _, lag in stages)
 
     def slot(s, carry):
+        @pl.when(s == 1)
+        def _():
+            in_copy(1).wait()
+            norm_half(1)
+
+        @pl.when((s >= 2) & (s < n_q + 4))
+        def _():
+            project_tile(s - 2, 1)
+
         @pl.when(s < 2 * n_seq + 2)
         def _():
             attend(s)
@@ -555,24 +530,37 @@
     lax.fori_loop(0, n_seq, drain, 0)
 
 
-def attend_and_project(prefix_len, q3, kn, vn, kc, vc, x2, w_o):
+def block(prefix_len, gain, q_gain, k_gain, x2, w_q, w_k, w_v, kc, vc, w_o):
     rows, d_model = x2.shape
     n_seq, cache_rows, _ = kc.shape
     n_part = 4
     width = d_model // (2 * n_part)
-    new_rows = kn.shape[0] // n_seq
-    tile = min(2048, cache_rows)
-    any_spec = pl.BlockSpec(memory_space=pl.ANY)
+    n_q = w_q.shape[1] // 256
+    new_rows = 2 * rows // n_seq
+    tile = min(2048, cache_rows // 2)
+    half_dim = HEAD_DIM // 2
+    freq = 1.0 / (1000000.0 ** (np.arange(half_dim, dtype=np.float64) * 2.0 / HEAD_DIM))
+    freq = jnp.asarray(np.concatenate([freq, freq])[None], jnp.float32)
+    hbm = pl.BlockSpec(memory_space=pl.ANY)
     vmem = pl.BlockSpec(memory_space=pltpu.VMEM)
     f32, bf16 = jnp.float32, jnp.bfloat16
     sems = pltpu.SemaphoreType.DMA
     piece = (32, width)
     return pl.pallas_call(
         functools.partial(block_kernel, tile=tile),
-        out_shape=pltpu.VMEM((rows, d_model), bf16),
-        in_specs=[pl.BlockSpec(memory_space=pltpu.SMEM), vmem, vmem, vmem, any_spec, any_spec, any_spec, any_spec],
-        out_specs=vmem,
+        out_shape=(
+            pltpu.VMEM((rows, d_model), bf16),
+            pltpu.VMEM((2 * rows, 128), bf16),
+            pltpu.VMEM((2 * rows, 128), bf16),
+        ),
+        in_specs=[pl.BlockSpec(memory_space=pltpu.SMEM), vmem, vmem, vmem, vmem, hbm, hbm, hbm, hbm, hbm, hbm, hbm],
+        out_specs=(vmem, vmem, vmem),
         scratch_shapes=[
+            pltpu.VMEM((n_q, rows, 256), bf16),
+            pltpu.VMEM((n_q + 2, d_model, 256), bf16),
+            pltpu.VMEM((rows, 128), f32),
+            pltpu.VMEM((rows, 128), f32),
+            pltpu.VMEM((rows, 128), f32),
             pltpu.VMEM((2, cache_rows, 128), bf16),
             pltpu.VMEM((2, cache_rows, 128), bf16),
             pltpu.VMEM((256, 256), bf16),
@@ -594,6 +582,8 @@
             pltpu.VMEM((n_seq, n_part, *piece), f32),
             pltpu.VMEM((n_seq, 4, n_part, *piece), f32),
             sems((2,)),
+            sems((n_q + 2,)),
+            sems((2,)),
             sems((2,)),
             sems((n_part,)),
             sems((n_seq,)),
@@ -603,23 +593,22 @@
             sems((n_seq, 2, n_part)),
         ],
         compiler_params=pltpu.CompilerParams(
-            collective_id=0, has_side_effects=True, vmem_limit_bytes=57 * 1024 * 1024
+            collective_id=0, has_side_effects=True, vmem_limit_bytes=int(58.5 * 1024 * 1024)
         ),
         cost_estimate=pl.CostEstimate(
             flops=4 * n_seq * cache_rows * 256 * 256, bytes_accessed=60 << 20, transcendentals=n_seq * cache_rows * 256
         ),
-        name="attend_and_project",
-    )(prefix_len, q3, kn, vn, kc, vc, x2, w_o)
+        name="block",
+    )(prefix_len, gain, q_gain, k_gain, freq, x2, w_q, w_k, w_v, kc, vc, w_o)
 
 
 def solution(mesh):
     def per_device(hidden, prefix_len, k_cache, v_cache, attn_norm, w_q, w_k, w_v, w_o, q_norm, k_norm):
         n_seq, n_new, d_model = hidden.shape
         x2 = hidden.reshape(n_seq * n_new, d_model)
-        q3, k_rows, v_rows = project(prefix_len, x2, attn_norm, w_q, w_k, w_v, q_norm, k_norm)
-        out = attend_and_project(
-            prefix_len, q3, k_rows, v_rows,
-            k_cache.reshape(n_seq, -1, HEAD_DIM), v_cache.reshape(n_seq, -1, HEAD_DIM), x2, w_o,
+        out, k_rows, v_rows = block(
+            prefix_len, attn_norm, q_norm, k_norm, x2, w_q, w_k, w_v,
+            k_cache.reshape(n_seq, -1, HEAD_DIM), v_cache.reshape(n_seq, -1, HEAD_DIM), w_o,
         )
         new_shape = (n_seq, n_new, 2, HEAD_DIM)
         return out.reshape(hidden.shape), k_rows.reshape(new_shape), v_rows.reshape(new_shape)

time: 122 us -> 119 us (0.975)
  Pallas kernels: 119 us -> 114 us
  local copies, waits for them, and re-layouts: 2.02 us -> 3.42 us
    pallas_call x2 -> x1, Pallas kernels: 119 us -> 114 us  [block(): pl.pallas_call(functools.partial(block_kernel, tile=tile), out_shape=(plt...]
    unnamed x1 -> x3, local copies, waits for them, and re-layouts: 2.02 us -> 3.42 us
where the time goes in v5:
time: 119 us
  Pallas kernels  114 us (96%)
  local copies, waits for them, and re-layouts  3.42 us (3%)
    pallas_call x1, Pallas kernels, block(): pl.pallas_call(functools.partial(block_kernel, tile=tile), out_shape=(plt...  114 us
    unnamed x3, local copies, waits for them, and re-layouts  3.42 us

profile of v5, /device:TPU:1, one launch (start us, length us, event | category | flops | bytes accessed | tf_op | source)
XLA Modules:
  0.0 118.5 jit_solution(14642762933722227010)
XLA Ops:
  0.6 114.5 %block.1 = (bf16[512,4096]{1,0:T(8,128)(2,1)S(1)}, bf16[1024,128]{1,0:T(8,128)(2,1)S(1)}, bf16[1024,128]{1,0:T(8,128)(2,1)S(1)}) custom-call(s32[8]{0:T(128)} %len_ref.1, bf16[4096]{0:T(1024)(128)(2,1)} %gain.1, bf16[128]{0:T(256)(128)(2,1)} %q_gain.1, bf16[128]{0:T(256)(128)(2,1)} %k_gain.1, f32[1,128]{1,0:T(1,128)} %constant.2.clone.freq, ...), custom_call_target="tpu_custom_call" | custom-call | flops 17179869184 | bytes 62914560 | tf_op jit(solution)/shard_map/block/pallas_call | solution.py:549
  115.1 2.0 %copy.18 = bf16[8,64,4096]{2,1,0:T(8,128)(2,1)} copy(bf16[8,64,4096]{2,1,0:T(8,128)(2,1)S(1)} %bitcast.6) | data formatting | bytes 8388608
  117.1 0.7 copy.19
  117.8 0.7 copy.20

commit v6 on v5

--- a/solution.py
+++ b/solution.py
@@ -468,9 +468,9 @@
                 out_ref[rows, col : col + width] = full[j, q, p].astype(jnp.bfloat16)
 
     stages = [
-        (stage_a1, 1), (stage_a2, 2), (stage_a3, 1), (stage_b1, 3), (stage_b2, 2), (stage_c0, 2),
-        (functools.partial(stage_c, d=1), 2), (functools.partial(stage_c, d=2), 3), (functools.partial(stage_c, d=3), 2),
-        (stage_over, 5), (stage_out, 5),
+        (stage_a1, 1), (stage_a2, 1), (stage_a3, 1), (stage_b1, 1), (stage_b2, 1), (stage_c0, 1),
+        (functools.partial(stage_c, d=1), 1), (functools.partial(stage_c, d=2), 1), (functools.partial(stage_c, d=3), 2),
+        (stage_over, 5), (stage_out, 6),
     ]
     n_slots = 2 * n_seq + 2 + sum(lag for _, lag in stages)
 
@@ -488,10 +488,10 @@
         def _():
             attend(s)
 
-        after = 3 + sum(lag for _, lag in stages)
-        for stage_fn, lag in reversed(stages):
+        after = 3
+        for stage_fn, lag in stages:
+            after += lag
             t = s - after
-            after -= lag
 
             @pl.when((t >= 0) & (t % 2 == 0) & (t < 2 * n_seq))
             def _():

time: 119 us -> 121 us (1.017)
  Pallas kernels: 114 us -> 116 us
    pallas_call x1, Pallas kernels: 114 us -> 116 us  [block(): pl.pallas_call(functools.partial(block_kernel, tile=tile), out_shape=(plt...]
where the time goes in v6:
time: 121 us; the launch traced here: 120 us
  Pallas kernels  116 us (96%)
  local copies, waits for them, and re-layouts  3.42 us (3%)
    pallas_call x1, Pallas kernels, block(): pl.pallas_call(functools.partial(block_kernel, tile=tile), out_shape=(plt...  116 us
    unnamed x3, local copies, waits for them, and re-layouts  3.42 us

profile of v6, /device:TPU:1, one launch (start us, length us, event | category | flops | bytes accessed | tf_op | source)
XLA Modules:
  0.0 120.1 jit_solution(8669433690948462611)
XLA Ops:
  0.6 116.1 %block.1 = (bf16[512,4096]{1,0:T(8,128)(2,1)S(1)}, bf16[1024,128]{1,0:T(8,128)(2,1)S(1)}, bf16[1024,128]{1,0:T(8,128)(2,1)S(1)}) custom-call(s32[8]{0:T(128)} %len_ref.1, bf16[4096]{0:T(1024)(128)(2,1)} %gain.1, bf16[128]{0:T(256)(128)(2,1)} %q_gain.1, bf16[128]{0:T(256)(128)(2,1)} %k_gain.1, f32[1,128]{1,0:T(1,128)} %constant.2.clone.freq, ...), custom_call_target="tpu_custom_call" | custom-call | flops 17179869184 | bytes 62914560 | tf_op jit(solution)/shard_map/block/pallas_call | solution.py:549
  116.7 2.0 %copy.18 = bf16[8,64,4096]{2,1,0:T(8,128)(2,1)} copy(bf16[8,64,4096]{2,1,0:T(8,128)(2,1)S(1)} %bitcast.6) | data formatting | bytes 8388608
  118.7 0.7 copy.19
  119.4 0.7 copy.20

commit v7 on v5

--- a/solution.py
+++ b/solution.py
@@ -52,9 +52,11 @@
         cols = pl.ds(pl.multiple_of(n_part * width * core + width * p, width), width)
         return pltpu.make_async_copy(wo_hbm.at[:, cols], wo.at[p], wo_sem.at[p])
 
+    owner = jnp.clip(z - 1, 0, 1)
+
     def x_copy(j):
         rows = pl.ds(pl.multiple_of(64 * j + 32 * y, 32), 32)
-        cols = pl.ds(pl.multiple_of(n_part * width * core + width * z, width), width)
+        cols = pl.ds(pl.multiple_of(n_part * width * core + 2 * width * owner, 2 * width), 2 * width)
         return pltpu.make_async_copy(x_hbm.at[rows, cols], xs.at[j], xs_sem.at[j])
 
     def in_copy(half):
@@ -363,12 +365,12 @@
 
         @pl.when(z == 0)
         def _():
-            for p in range(last, 0, -1):
+            for p in (2, 3, 0, 1):
                 b_right(j, p).start()
 
         @pl.when(z == last)
         def _():
-            for p in range(last):
+            for p in (0, 1, 2, 3):
                 b_left(j, p).start()
 
     def pass_right(j, p):
@@ -384,73 +386,83 @@
     def stage_b1(j):
         @pl.when(z == 1)
         def _():
+            pass_right(j, 2)
             pass_right(j, 3)
-            pass_right(j, 2)
 
         @pl.when(z == 2)
         def _():
             pass_left(j, 0)
             pass_left(j, 1)
 
-    def stage_b2(j):
-        @pl.when(z == 2)
-        def _():
-            pass_right(j, 3)
-
-        @pl.when(z == 1)
-        def _():
-            pass_left(j, 0)
+    def spread(j, p):
+        c_over(j, c, p).start()
+        c_mate(j, c, 0, p).start()
 
     def stage_c0(j):
         x_copy(j).wait()
 
-        @pl.when(z > 0)
-        def _():
-            b_right(j, z).wait_recv()
-            prod[j, z] = prod[j, z] + from_l[j, z]
-
-        @pl.when(z < last)
-        def _():
-            b_left(j, z).wait_recv()
-            prod[j, z] = prod[j, z] + from_r[j, z]
-
-        full[j, c, z] = prod[j, z] + xs[j].astype(jnp.float32)
-
-        @pl.when(z < last)
-        def _():
-            c_right(j, z).start()
-
-        @pl.when(z > 0)
-        def _():
-            c_left(j, z).start()
-
-        c_over(j, c, z).start()
-        c_mate(j, c, 0, z).start()
-
-    def stage_c(j, d):
-        @pl.when(z - d >= 0)
-        def _():
-            p = z - d
-            c_right(j, p).wait_recv()
-
-            @pl.when(z < last)
-            def _():
-                c_right(j, p).start()
-
-            c_over(j, c, p).start()
-            c_mate(j, c, 0, p).start()
-
-        @pl.when(z + d <= last)
-        def _():
-            p = z + d
-            c_left(j, p).wait_recv()
-
-            @pl.when(z > 0)
-            def _():
-                c_left(j, p).start()
-
-            c_over(j, c, p).start()
-            c_mate(j, c, 0, p).start()
+        def finish(p):
+            b_right(j, p).wait_recv()
+            b_left(j, p).wait_recv()
+            x = xs[j, :, width * (p % 2) : width * (p % 2) + width].astype(jnp.float32)
+            full[j, c, p] = prod[j, p] + from_l[j, p] + from_r[j, p] + x
+            c_right(j, p).start()
+            c_left(j, p).start()
+            spread(j, p)
+
+        @pl.when(z == 1)
+        def _():
+            finish(0)
+            finish(1)
+
+        @pl.when(z == 2)
+        def _():
+            finish(2)
+            finish(3)
+
+    def from_right(j, p, onward):
+        c_left(j, p).wait_recv()
+        if onward:
+            c_left(j, p).start()
+        spread(j, p)
+
+    def from_left(j, p, onward):
+        c_right(j, p).wait_recv()
+        if onward:
+            c_right(j, p).start()
+        spread(j, p)
+
+    def stage_c1(j):
+        @pl.when(z == 0)
+        def _():
+            from_right(j, 0, False)
+            from_right(j, 1, False)
+
+        @pl.when(z == 1)
+        def _():
+            from_right(j, 2, True)
+            from_right(j, 3, True)
+
+        @pl.when(z == 2)
+        def _():
+            from_left(j, 0, True)
+            from_left(j, 1, True)
+
+        @pl.when(z == 3)
+        def _():
+            from_left(j, 2, False)
+            from_left(j, 3, False)
+
+    def stage_c2(j):
+        @pl.when(z == 0)
+        def _():
+            from_right(j, 2, False)
+            from_right(j, 3, False)
+
+        @pl.when(z == 3)
+        def _():
+            from_left(j, 0, False)
+            from_left(j, 1, False)
 
     def stage_over(j):
         for p in range(n_part):
@@ -468,9 +480,8 @@
                 out_ref[rows, col : col + width] = full[j, q, p].astype(jnp.bfloat16)
 
     stages = [
-        (stage_a1, 1), (stage_a2, 2), (stage_a3, 1), (stage_b1, 3), (stage_b2, 2), (stage_c0, 2),
-        (functools.partial(stage_c, d=1), 2), (functools.partial(stage_c, d=2), 3), (functools.partial(stage_c, d=3), 2),
-        (stage_over, 5), (stage_out, 5),
+        (stage_a1, 1), (stage_a2, 2), (stage_a3, 1), (stage_b1, 2), (stage_c0, 1), (stage_c1, 2), (stage_c2, 1),
+        (stage_over, 6), (stage_out, 2),
     ]
     n_slots = 2 * n_seq + 2 + sum(lag for _, lag in stages)
 
@@ -506,19 +517,19 @@
         a2(j).wait_send()
         a3(j, core).wait_send()
         for p in range(n_part):
-            @pl.when(z < p)
+            @pl.when((z == 0) | ((z == 1) & (p >= 2)))
             def _():
                 b_right(j, p).wait_send()
 
-            @pl.when(z > p)
+            @pl.when((z == 3) | ((z == 2) & (p < 2)))
             def _():
                 b_left(j, p).wait_send()
 
-            @pl.when((z >= p) & (z < last))
+            @pl.when((z == 2) | ((z == 1) & (p < 2)))
             def _():
                 c_right(j, p).wait_send()
 
-            @pl.when((z <= p) & (z > 0))
+            @pl.when((z == 1) | ((z == 2) & (p >= 2)))
             def _():
                 c_left(j, p).wait_send()
 
@@ -571,7 +582,7 @@
             pltpu.VMEM((8, 256), f32),
             pltpu.VMEM((8, 256), f32),
             pltpu.VMEM((n_part, w_o.shape[0], width), bf16),
-            pltpu.VMEM((n_seq, *piece), bf16),
+            pltpu.VMEM((n_seq, 32, 2 * width), bf16),
             pltpu.VMEM((n_seq, 2, 136, 256), f32),
             pltpu.VMEM((n_seq, 136, 256), f32),
             pltpu.VMEM((n_seq, 2, 136, 128), f32),
@@ -602,14 +613,39 @@
     )(prefix_len, gain, q_gain, k_gain, freq, x2, w_q, w_k, w_v, kc, vc, w_o)
 
 
+def store_kernel(out_in, k_in, v_in, out_hbm, k_hbm, v_hbm, sem):
+    copies = [
+        pltpu.make_async_copy(src, dst, sem.at[i])
+        for i, (src, dst) in enumerate(((out_in, out_hbm), (k_in, k_hbm), (v_in, v_hbm)))
+    ]
+    for copy in copies:
+        copy.start()
+    for copy in copies:
+        copy.wait()
+
+
+def store(*arrays):
+    hbm = pl.BlockSpec(memory_space=pl.ANY)
+    return pl.pallas_call(
+        store_kernel,
+        out_shape=tuple(jax.ShapeDtypeStruct(a.shape, a.dtype) for a in arrays),
+        in_specs=[hbm] * 3,
+        out_specs=(hbm,) * 3,
+        scratch_shapes=[pltpu.SemaphoreType.DMA((3,))],
+        compiler_params=pltpu.CompilerParams(vmem_limit_bytes=1024 * 1024),
+        name="store",
+    )(*arrays)
+
+
 def solution(mesh):
     def per_device(hidden, prefix_len, k_cache, v_cache, attn_norm, w_q, w_k, w_v, w_o, q_norm, k_norm):
         n_seq, n_new, d_model = hidden.shape
         x2 = hidden.reshape(n_seq * n_new, d_model)
-        out, k_rows, v_rows = block(
+        results = block(
             prefix_len, attn_norm, q_norm, k_norm, x2, w_q, w_k, w_v,
             k_cache.reshape(n_seq, -1, HEAD_DIM), v_cache.reshape(n_seq, -1, HEAD_DIM), w_o,
         )
+        out, k_rows, v_rows = store(*results)
         new_shape = (n_seq, n_new, 2, HEAD_DIM)
         return out.reshape(hidden.shape), k_rows.reshape(new_shape), v_rows.reshape(new_shape)
 

time: 119 us -> 113 us (0.950)
  local copies, waits for them, and re-layouts: 3.42 us -> 0 us
  Pallas kernels: 114 us -> 112 us
    pallas_call x1, Pallas kernels: 114 us -> 110 us  [block(): pl.pallas_call(functools.partial(block_kernel, tile=tile), out_shape=(plt...]
    unnamed x3 -> x0, local copies, waits for them, and re-layouts: 3.42 us -> none
    pallas_call x0 -> x1, Pallas kernels: none -> 2.19 us  [store(): pl.pallas_call(store_kernel, out_shape=tuple((jax.ShapeDtypeStruct(a.shap...]
where the time goes in v7:
time: 113 us
  Pallas kernels  112 us (99%)
    pallas_call x1, Pallas kernels, block(): pl.pallas_call(functools.partial(block_kernel, tile=tile), out_shape=(plt...  110 us

profile of v7, /device:TPU:1, one launch (start us, length us, event | category | flops | bytes accessed | tf_op | source)
XLA Modules:
  0.0 113.1 jit_solution(12678564104919209120)
XLA Ops:
  0.6 110.3 %block.1 = (bf16[512,4096]{1,0:T(8,128)(2,1)S(1)}, bf16[1024,128]{1,0:T(8,128)(2,1)S(1)}, bf16[1024,128]{1,0:T(8,128)(2,1)S(1)}) custom-call(s32[8]{0:T(128)} %len_ref.1, bf16[4096]{0:T(1024)(128)(2,1)} %gain.1, bf16[128]{0:T(256)(128)(2,1)} %q_gain.1, bf16[128]{0:T(256)(128)(2,1)} %k_gain.1, f32[1,128]{1,0:T(1,128)} %constant.2.clone.freq, ...), custom_call_target="tpu_custom_call" | custom-call | flops 17179869184 | bytes 62914560 | tf_op jit(solution)/shard_map/block/pallas_call | solution.py:560
  110.9 2.2 %store.1 = (bf16[512,4096]{1,0:T(8,128)(2,1)}, bf16[1024,128]{1,0:T(8,128)(2,1)}, bf16[1024,128]{1,0:T(8,128)(2,1)}) custom-call(bf16[512,4096]{1,0:T(8,128)(2,1)S(1)} %get-tuple-element.9.out_in, bf16[1024,128]{1,0:T(8,128)(2,1)S(1)} %get-tuple-element.10.k_in, bf16[1024,128]{1,0:T(8,128)(2,1)S(1)} %get-tuple-element.11.v_in), custom_call_target="tpu_custom_call" | custom-call | tf_op jit(solution)/shard_map/store/pallas_call | solution.py:629

commit v8 on v7

--- a/solution.py
+++ b/solution.py
@@ -17,10 +17,10 @@
 def block_kernel(
     len_ref, gain, q_gain, k_gain, freq, x_hbm, wq_hbm, wk_hbm, wv_hbm, kc_hbm, vc_hbm, wo_hbm,
     out_ref, kn_ref, vn_ref,
-    q_ref, w_buf, cos_t, sin_t, turn, kbuf, vbuf, qt, s_buf, sn_buf, acc, top_buf, run_top, run_sum,
+    q_ref, w_buf, cos_t, sin_t, turn, mine, theirs, kbuf, vbuf, qt, s_buf, sn_buf, acc, top_buf, run_top, run_sum,
     wo, xs, part, got1, chip, got2, ob, prod, from_l, from_r, full,
     x_sem, w_sem, k_sem, v_sem, wo_sem, xs_sem, a1s, a1r, a2s, a2r, a3s, a3r,
-    brs, brr, bls, blr, crs, crr, cls, clr, cys, cyr, cps, cpr, *, tile,
+    shs, shr, brs, brr, bls, blr, crs, crr, cls, clr, cys, cyr, cps, cpr, *, tile,
 ):
     dp, z, c = lax.axis_index("dp"), lax.axis_index("tp"), lax.axis_index("cp")
     y, core = c // 2, c % 2
@@ -109,24 +109,35 @@
     q_gain_row = q_gain[...].astype(jnp.float32).reshape(1, 128)
     k_gain_row = k_gain[...].astype(jnp.float32).reshape(1, 128)
 
-    def project_tile(i, half):
-        sel = slice(half * half_rows, (half + 1) * half_rows)
+    def half_sel(half):
+        return slice(half * half_rows, (half + 1) * half_rows)
+
+    def compute_tile(i, half):
+        sel = half_sel(half)
         lin = jnp.dot(out_ref[sel, :], w_buf[i], preferred_element_type=jnp.float32).astype(jnp.bfloat16)
         lin = lin.astype(jnp.float32)
         head_gain = jnp.where(i < n_q, q_gain_row, k_gain_row)
+        vals = []
         for u in range(2):
             raw = lin[:, 128 * u : 128 * u + 128]
             mean_sq = jnp.mean(raw * raw, axis=-1, keepdims=True)
             t = raw * lax.rsqrt(mean_sq + 1e-6) * head_gain
             t = t * cos_t[sel, :] + pltpu.roll(t, 64, 1) * sin_t[sel, :]
-
-            @pl.when(i < n_q)
-            def _():
-                q_ref[i, sel, 128 * u : 128 * u + 128] = t.astype(jnp.bfloat16)
-
-            @pl.when(i >= n_q)
-            def _():
-                turn[pl.ds(u, half_rows, stride=2), :] = jnp.where(i == n_q, t, raw)
+            vals.append(jnp.where(i == n_q + 1, raw, t))
+        return vals
+
+    def store_tile(i, half, vals):
+        sel = half_sel(half)
+
+        @pl.when(i < n_q)
+        def _():
+            for u in range(2):
+                q_ref[i, sel, 128 * u : 128 * u + 128] = vals[u].astype(jnp.bfloat16)
+
+        @pl.when(i >= n_q)
+        def _():
+            for u in range(2):
+                turn[pl.ds(u, half_rows, stride=2), :] = vals[u]
 
         new_rows = slice(half * rows, (half + 1) * rows)
 
@@ -137,6 +148,23 @@
         @pl.when(i == n_q + 1)
         def _():
             vn_ref[new_rows, :] = turn[...].astype(jnp.bfloat16)
+
+    n_share = (n_q + 2) // 2
+
+    def share(m):
+        return send(mine.at[m], theirs.at[m], shs.at[m], shr.at[m], z, mate)
+
+    def share_tile(m):
+        i = 2 * m + core
+        vals = compute_tile(i, 1)
+        for u in range(2):
+            mine[m, :, 128 * u : 128 * u + 128] = vals[u]
+        share(m).start()
+        store_tile(i, 1, vals)
+
+    def take_tile(m):
+        share(m).wait_recv()
+        store_tile(2 * m + 1 - core, 1, [theirs[m, :, 128 * u : 128 * u + 128] for u in range(2)])
 
     in_copy(0).wait()
     for copy in w_copies:
@@ -147,7 +175,7 @@
 
     def first_tile(i, carry):
         pltpu.make_async_copy(w_buf.at[i], w_buf.at[i], w_sem.at[i]).wait()
-        project_tile(i, 0)
+        store_tile(i, 0, compute_tile(i, 0))
         return carry
 
     lax.fori_loop(0, n_q + 2, first_tile, 0)
@@ -480,8 +508,8 @@
                 out_ref[rows, col : col + width] = full[j, q, p].astype(jnp.bfloat16)
 
     stages = [
-        (stage_a1, 1), (stage_a2, 2), (stage_a3, 1), (stage_b1, 2), (stage_c0, 1), (stage_c1, 2), (stage_c2, 1),
-        (stage_over, 6), (stage_out, 2),
+        (stage_a1, 1), (stage_a2, 2), (stage_a3, 1), (stage_b1, 2), (stage_c0, 2), (stage_c1, 1), (stage_c2, 1),
+        (stage_over, 3), (stage_out, 2),
     ]
     n_slots = 2 * n_seq + 2 + sum(lag for _, lag in stages)
 
@@ -491,9 +519,13 @@
             in_copy(1).wait()
             norm_half(1)
 
-        @pl.when((s >= 2) & (s < n_q + 4))
-        def _():
-            project_tile(s - 2, 1)
+        @pl.when((s >= 2) & (s < 2 + n_share))
+        def _():
+            share_tile(s - 2)
+
+        @pl.when((s >= 4) & (s < 4 + n_share))
+        def _():
+            take_tile(s - 4)
 
         @pl.when(s < 2 * n_seq + 2)
         def _():
@@ -538,6 +570,8 @@
             c_mate(j, over, 1, p).wait_send()
         return carry
 
+    for m in range(n_share):
+        share(m).wait_send()
     lax.fori_loop(0, n_seq, drain, 0)
 
 
@@ -548,6 +582,7 @@
     width = d_model // (2 * n_part)
     n_q = w_q.shape[1] // 256
     new_rows = 2 * rows // n_seq
+    n_share = (n_q + 2) // 2
     tile = min(2048, cache_rows // 2)
     half_dim = HEAD_DIM // 2
     freq = 1.0 / (1000000.0 ** (np.arange(half_dim, dtype=np.float64) * 2.0 / HEAD_DIM))
@@ -572,6 +607,8 @@
             pltpu.VMEM((rows, 128), f32),
             pltpu.VMEM((rows, 128), f32),
             pltpu.VMEM((rows, 128), f32),
+            pltpu.VMEM((n_share, rows // 2, 256), f32),
+            pltpu.VMEM((n_share, rows // 2, 256), f32),
             pltpu.VMEM((2, cache_rows, 128), bf16),
             pltpu.VMEM((2, cache_rows, 128), bf16),
             pltpu.VMEM((256, 256), bf16),
@@ -599,6 +636,7 @@
             sems((n_part,)),
             sems((n_seq,)),
             *[sems((n_seq,))] * 6,
+            *[sems((n_share,))] * 2,
             *[sems((n_seq, n_part))] * 10,
             sems((n_seq, 2, n_part)),
             sems((n_seq, 2, n_part)),

time: 113 us -> 108 us (0.956)
  Pallas kernels: 112 us -> 107 us
    pallas_call x1, Pallas kernels: 110 us -> 105 us  [block(): pl.pallas_call(functools.partial(block_kernel, tile=tile), out_shape=(plt...]
where the time goes in v8:
time: 108 us
  Pallas kernels  107 us (99%)
    pallas_call x1, Pallas kernels, block(): pl.pallas_call(functools.partial(block_kernel, tile=tile), out_shape=(plt...  105 us
    pallas_call x1, Pallas kernels, store(): pl.pallas_call(store_kernel, out_shape=tuple((jax.ShapeDtypeStruct(a.shap...  2.19 us

profile of v8, /device:TPU:1, one launch (start us, length us, event | category | flops | bytes accessed | tf_op | source)
XLA Modules:
  0.0 108.1 jit_solution(16141931105341499317)
XLA Ops:
  0.6 105.3 %block.1 = (bf16[512,4096]{1,0:T(8,128)(2,1)S(1)}, bf16[1024,128]{1,0:T(8,128)(2,1)S(1)}, bf16[1024,128]{1,0:T(8,128)(2,1)S(1)}) custom-call(s32[8]{0:T(128)} %len_ref.1, bf16[4096]{0:T(1024)(128)(2,1)} %gain.1, bf16[128]{0:T(256)(128)(2,1)} %q_gain.1, bf16[128]{0:T(256)(128)(2,1)} %k_gain.1, f32[1,128]{1,0:T(1,128)} %constant.2.clone.freq, ...), custom_call_target="tpu_custom_call" | custom-call | flops 17179869184 | bytes 62914560 | tf_op jit(solution)/shard_map/block/pallas_call | solution.py:595
  105.9 2.2 %store.1 = (bf16[512,4096]{1,0:T(8,128)(2,1)}, bf16[1024,128]{1,0:T(8,128)(2,1)}, bf16[1024,128]{1,0:T(8,128)(2,1)}) custom-call(bf16[512,4096]{1,0:T(8,128)(2,1)S(1)} %get-tuple-element.9.out_in, bf16[1024,128]{1,0:T(8,128)(2,1)S(1)} %get-tuple-element.10.k_in, bf16[1024,128]{1,0:T(8,128)(2,1)S(1)} %get-tuple-element.11.v_in), custom_call_target="tpu_custom_call" | custom-call | tf_op jit(solution)/shard_map/store/pallas_call | solution.py:667

commit v9 on v8

--- a/solution.py
+++ b/solution.py
@@ -82,8 +82,8 @@
     def _():
         pl.semaphore_signal(barrier, inc=1, device_id=(dp, z + 1, c), device_id_type=MESH)
 
-    rope_lane = lax.broadcasted_iota(jnp.int32, (n_tok, 128), 1)
-    rope_token = lax.broadcasted_iota(jnp.int32, (n_tok, 128), 0)
+    rope_lane = lax.broadcasted_iota(jnp.int32, (n_tok, HEAD_DIM), 1)
+    rope_token = lax.broadcasted_iota(jnp.int32, (n_tok, HEAD_DIM), 0)
 
     def rope_rows(b, carry):
         angle = (rope_token + len_ref[b]).astype(jnp.float32) * freq[...]
@@ -106,8 +106,8 @@
 
         lax.fori_loop(0, half_rows // 32, norm_rows, 0)
 
-    q_gain_row = q_gain[...].astype(jnp.float32).reshape(1, 128)
-    k_gain_row = k_gain[...].astype(jnp.float32).reshape(1, 128)
+    q_gain_row = q_gain[...].astype(jnp.float32).reshape(1, HEAD_DIM)
+    k_gain_row = k_gain[...].astype(jnp.float32).reshape(1, HEAD_DIM)
 
     def half_sel(half):
         return slice(half * half_rows, (half + 1) * half_rows)
@@ -119,7 +119,7 @@
         head_gain = jnp.where(i < n_q, q_gain_row, k_gain_row)
         vals = []
         for u in range(2):
-            raw = lin[:, 128 * u : 128 * u + 128]
+            raw = lin[:, HEAD_DIM * u : HEAD_DIM * u + HEAD_DIM]
             mean_sq = jnp.mean(raw * raw, axis=-1, keepdims=True)
             t = raw * lax.rsqrt(mean_sq + 1e-6) * head_gain
             t = t * cos_t[sel, :] + pltpu.roll(t, 64, 1) * sin_t[sel, :]
@@ -132,7 +132,7 @@
         @pl.when(i < n_q)
         def _():
             for u in range(2):
-                q_ref[i, sel, 128 * u : 128 * u + 128] = vals[u].astype(jnp.bfloat16)
+                q_ref[i, sel, HEAD_DIM * u : HEAD_DIM * u + HEAD_DIM] = vals[u].astype(jnp.bfloat16)
 
         @pl.when(i >= n_q)
         def _():
@@ -158,13 +158,13 @@
         i = 2 * m + core
         vals = compute_tile(i, 1)
         for u in range(2):
-            mine[m, :, 128 * u : 128 * u + 128] = vals[u]
+            mine[m, :, HEAD_DIM * u : HEAD_DIM * u + HEAD_DIM] = vals[u]
         share(m).start()
         store_tile(i, 1, vals)
 
     def take_tile(m):
         share(m).wait_recv()
-        store_tile(2 * m + 1 - core, 1, [theirs[m, :, 128 * u : 128 * u + 128] for u in range(2)])
+        store_tile(2 * m + 1 - core, 1, [theirs[m, :, HEAD_DIM * u : HEAD_DIM * u + HEAD_DIM] for u in range(2)])
 
     in_copy(0).wait()
     for copy in w_copies:
@@ -193,16 +193,16 @@
     def _():
         pl.semaphore_wait(barrier, 4)
 
-    sub16 = lax.broadcasted_iota(jnp.int32, (16, 128), 0) & 1
+    sub16 = lax.broadcasted_iota(jnp.int32, (16, HEAD_DIM), 0) & 1
     even_rows = jnp.where(sub16 == 0, 1.0, 0.0).astype(jnp.bfloat16)
     odd_rows = jnp.where(sub16 == 0, 0.0, 1.0).astype(jnp.bfloat16)
     sub8 = lax.broadcasted_iota(jnp.int32, (8, 256), 0) & 1
 
     def split_rows(k):
         n = k.shape[0]
-        k3 = k.reshape(n // 16, 16, 128)
+        k3 = k.reshape(n // 16, 16, HEAD_DIM)
         return jnp.concatenate(
-            [(k3 * even_rows[None]).reshape(n, 128), (k3 * odd_rows[None]).reshape(n, 128)], axis=1
+            [(k3 * even_rows[None]).reshape(n, HEAD_DIM), (k3 * odd_rows[None]).reshape(n, HEAD_DIM)], axis=1
         )
 
     def split_lanes(v):
@@ -211,7 +211,7 @@
         even = jnp.where(lane == 0, 1.0, 0.0).astype(jnp.bfloat16)
         odd = jnp.where(lane == 0, 0.0, 1.0).astype(jnp.bfloat16)
         vt = v.T.reshape(8, 16, n)
-        return jnp.concatenate([(vt * even[None]).reshape(128, n), (vt * odd[None]).reshape(128, n)], axis=0)
+        return jnp.concatenate([(vt * even[None]).reshape(HEAD_DIM, n), (vt * odd[None]).reshape(HEAD_DIM, n)], axis=0)
 
     def scores(k):
         return jnp.dot(split_rows(k), qt[...], preferred_element_type=jnp.float32)
@@ -229,11 +229,11 @@
         q_rows = pl.multiple_of(64 * b, 64)
         for h in range(2):
             blocks = [
-                q_ref[h * 2 + g // 2, pl.ds(q_rows + th * 32, 32), (g % 2) * 128 : (g % 2) * 128 + 128]
+                q_ref[h * 2 + g // 2, pl.ds(q_rows + th * 32, 32), (g % 2) * HEAD_DIM : (g % 2) * HEAD_DIM + HEAD_DIM]
                 for th in range(2)
                 for g in range(4)
             ]
-            qt[h * 128 : h * 128 + 128, :] = jnp.concatenate(blocks, axis=0).T
+            qt[h * HEAD_DIM : h * HEAD_DIM + HEAD_DIM, :] = jnp.concatenate(blocks, axis=0).T
         run_top[...] = jnp.full((8, 256), MASKED, jnp.float32)
         k_copy(b).wait()
 
@@ -248,7 +248,7 @@
     def score_end(b):
         key = lax.broadcasted_iota(jnp.int32, (n_new, 256), 0) // 2
         col = lax.broadcasted_iota(jnp.int32, (n_new, 256), 1)
-        token = (col // 128) * 32 + (col % 32)
+        token = (col // HEAD_DIM) * 32 + (col % 32)
         token = jnp.where(c == 3, token, -1)
         s_new = jnp.where(key <= token, scores(kn_ref[pl.ds(pl.multiple_of(n_new * b, n_new), n_new), :]), MASKED)
         sn_buf[...] = s_new
@@ -279,9 +279,9 @@
         total = run_sum[...]
         pad = jnp.zeros((6, 256), jnp.float32)
         for h in range(2):
-            part[b, h, 0:128, :] = acc[h * 128 : h * 128 + 128, :]
+            part[b, h, 0:HEAD_DIM, :] = acc[h * HEAD_DIM : h * HEAD_DIM + HEAD_DIM, :]
             total_h = jnp.sum(jnp.where(sub8 == h, total, 0.0), axis=0, keepdims=True)
-            part[b, h, 128:136, :] = jnp.concatenate([top_buf[h : h + 1, :], total_h, pad], axis=0)
+            part[b, h, HEAD_DIM:136, :] = jnp.concatenate([top_buf[h : h + 1, :], total_h, pad], axis=0)
         a1(b).start()
 
     def attend(s):
@@ -358,18 +358,18 @@
         return send(full.at[j, q, p], full.at[j, q, p], cps.at[j, u, p], cpr.at[j, u, p], z, mate)
 
     def merge(a, b):
-        top = jnp.maximum(a[128:129], b[128:129])
-        fa = jnp.exp2((a[128:129] - top) * EXP2_SCALE)
-        fb = jnp.exp2((b[128:129] - top) * EXP2_SCALE)
-        return a[0:128] * fa + b[0:128] * fb, top, a[129:130] * fa + b[129:130] * fb
+        top = jnp.maximum(a[HEAD_DIM:129], b[HEAD_DIM:129])
+        fa = jnp.exp2((a[HEAD_DIM:129] - top) * EXP2_SCALE)
+        fb = jnp.exp2((b[HEAD_DIM:129] - top) * EXP2_SCALE)
+        return a[0:HEAD_DIM] * fa + b[0:HEAD_DIM] * fb, top, a[129:130] * fa + b[129:130] * fb
 
     def stage_a1(j):
         a1(j).wait_recv()
         vals, top, total = merge(part[j, core], got1[j])
         for th in range(2):
-            sel = slice(128 * th, 128 * th + 128)
-            chip[j, th, 0:128] = vals[:, sel]
-            chip[j, th, 128:136] = jnp.concatenate([top[:, sel], total[:, sel], jnp.zeros((6, 128), jnp.float32)], axis=0)
+            sel = slice(HEAD_DIM * th, HEAD_DIM * th + HEAD_DIM)
+            chip[j, th, 0:HEAD_DIM] = vals[:, sel]
+            chip[j, th, HEAD_DIM:136] = jnp.concatenate([top[:, sel], total[:, sel], jnp.zeros((6, HEAD_DIM), jnp.float32)], axis=0)
         a2(j).start()
 
     def stage_a2(j):
@@ -596,21 +596,21 @@
         functools.partial(block_kernel, tile=tile),
         out_shape=(
             pltpu.VMEM((rows, d_model), bf16),
-            pltpu.VMEM((2 * rows, 128), bf16),
-            pltpu.VMEM((2 * rows, 128), bf16),
+            pltpu.VMEM((2 * rows, HEAD_DIM), bf16),
+            pltpu.VMEM((2 * rows, HEAD_DIM), bf16),
         ),
         in_specs=[pl.BlockSpec(memory_space=pltpu.SMEM), vmem, vmem, vmem, vmem, hbm, hbm, hbm, hbm, hbm, hbm, hbm],
         out_specs=(vmem, vmem, vmem),
         scratch_shapes=[
             pltpu.VMEM((n_q, rows, 256), bf16),
             pltpu.VMEM((n_q + 2, d_model, 256), bf16),
-            pltpu.VMEM((rows, 128), f32),
-            pltpu.VMEM((rows, 128), f32),
-            pltpu.VMEM((rows, 128), f32),
+            pltpu.VMEM((rows, HEAD_DIM), f32),
+            pltpu.VMEM((rows, HEAD_DIM), f32),
+            pltpu.VMEM((rows, HEAD_DIM), f32),
             pltpu.VMEM((n_share, rows // 2, 256), f32),
             pltpu.VMEM((n_share, rows // 2, 256), f32),
-            pltpu.VMEM((2, cache_rows, 128), bf16),
-            pltpu.VMEM((2, cache_rows, 128), bf16),
+            pltpu.VMEM((2, cache_rows, HEAD_DIM), bf16),
+            pltpu.VMEM((2, cache_rows, HEAD_DIM), bf16),
             pltpu.VMEM((256, 256), bf16),
             pltpu.VMEM((cache_rows, 256), f32),
             pltpu.VMEM((new_rows, 256), f32),
@@ -622,9 +622,9 @@
             pltpu.VMEM((n_seq, 32, 2 * width), bf16),
             pltpu.VMEM((n_seq, 2, 136, 256), f32),
             pltpu.VMEM((n_seq, 136, 256), f32),
-            pltpu.VMEM((n_seq, 2, 136, 128), f32),
-            pltpu.VMEM((n_seq, 136, 128), f32),
-            pltpu.VMEM((n_seq, 2, 128, 128), f32),
+            pltpu.VMEM((n_seq, 2, 136, HEAD_DIM), f32),
+            pltpu.VMEM((n_seq, 136, HEAD_DIM), f32),
+            pltpu.VMEM((n_seq, 2, HEAD_DIM, HEAD_DIM), f32),
             pltpu.VMEM((n_seq, n_part, *piece), f32),
             pltpu.VMEM((n_seq, n_part, *piece), f32),
             pltpu.VMEM((n_seq, n_part, *piece), f32),

time: 108 us -> 108 us (level)
  no operation moved by 1% of the time
where the time goes in v9:
time: 108 us
  Pallas kernels  107 us (99%)
    pallas_call x1, Pallas kernels, block(): pl.pallas_call(functools.partial(block_kernel, tile=tile), out_shape=(plt...  105 us
    pallas_call x1, Pallas kernels, store(): pl.pallas_call(store_kernel, out_shape=tuple((jax.ShapeDtypeStruct(a.shap...  2.19 us

profile of v9, /device:TPU:1, one launch (start us, length us, event | category | flops | bytes accessed | tf_op | source)
XLA Modules:
  0.0 108.1 jit_solution(16141931105341499317)
XLA Ops:
  0.6 105.3 %block.1 = (bf16[512,4096]{1,0:T(8,128)(2,1)S(1)}, bf16[1024,128]{1,0:T(8,128)(2,1)S(1)}, bf16[1024,128]{1,0:T(8,128)(2,1)S(1)}) custom-call(s32[8]{0:T(128)} %len_ref.1, bf16[4096]{0:T(1024)(128)(2,1)} %gain.1, bf16[128]{0:T(256)(128)(2,1)} %q_gain.1, bf16[128]{0:T(256)(128)(2,1)} %k_gain.1, f32[1,128]{1,0:T(1,128)} %constant.2.clone.freq, ...), custom_call_target="tpu_custom_call" | custom-call | flops 17179869184 | bytes 62914560 | tf_op jit(solution)/shard_map/block/pallas_call | solution.py:595
  105.9 2.2 %store.1 = (bf16[512,4096]{1,0:T(8,128)(2,1)}, bf16[1024,128]{1,0:T(8,128)(2,1)}, bf16[1024,128]{1,0:T(8,128)(2,1)}) custom-call(bf16[512,4096]{1,0:T(8,128)(2,1)S(1)} %get-tuple-element.9.out_in, bf16[1024,128]{1,0:T(8,128)(2,1)S(1)} %get-tuple-element.10.k_in, bf16[1024,128]{1,0:T(8,128)(2,1)S(1)} %get-tuple-element.11.v_in), custom_call_target="tpu_custom_call" | custom-call | tf_op jit(solution)/shard_map/store/pallas_call | solution.py:667

commit v10 on v9

--- a/solution.py
+++ b/solution.py
@@ -287,6 +287,17 @@
     def attend(s):
         b, first = s // 2, s % 2 == 0
 
+        def tiles(body, start, count):
+            def one(i, carry):
+                body(start + i)
+                return carry
+
+            lax.fori_loop(0, count, one, 0)
+
+        half = n_tiles // 2
+        start = jnp.where(b == 0, 0, (s % 2) * half)
+        count = jnp.where(b == 0, n_tiles, half)
+
         @pl.when(first)
         def _():
             fetch(b)
@@ -295,38 +306,31 @@
         def _():
             score_start(b)
 
-        @pl.when(first & (b > 0))
-        def _():
-            weigh_start(b - 1)
-
-        def tiles(body):
-            def one(i, carry):
-                body((s % 2) * (n_tiles // 2) + i)
-                return carry
-
-            lax.fori_loop(0, n_tiles // 2, one, 0)
-
-        @pl.when(b == 0)
-        def _():
-            tiles(lambda t: score_tile(b, t))
-
-        @pl.when((b > 0) & (b < n_seq))
+        @pl.when((first & (b > 1)) | (s == 1))
+        def _():
+            weigh_start(jnp.where(s == 1, 0, b - 1))
+
+        @pl.when((s == 0) | (b == 1))
+        def _():
+            tiles(lambda t: score_tile(b, t), start, count)
+
+        @pl.when((b > 1) & (b < n_seq))
         def _():
             def both(t):
                 weigh_tile(b - 1, t)
                 score_tile(b, t)
 
-            tiles(both)
-
-        @pl.when(b == n_seq)
-        def _():
-            tiles(lambda t: weigh_tile(b - 1, t))
-
-        @pl.when((s % 2 == 1) & (b > 0))
-        def _():
-            weigh_end(b - 1)
-
-        @pl.when((s % 2 == 1) & (b < n_seq))
+            tiles(both, start, half)
+
+        @pl.when((s == 1) | (b == n_seq))
+        def _():
+            tiles(lambda t: weigh_tile(jnp.where(s == 1, 0, b - 1), t), start, count)
+
+        @pl.when(((s % 2 == 1) & (b > 1)) | (s == 1))
+        def _():
+            weigh_end(jnp.where(s == 1, 0, b - 1))
+
+        @pl.when(((s % 2 == 1) & (b > 0) & (b < n_seq)) | (s == 0))
         def _():
             score_end(b)
 
@@ -514,18 +518,18 @@
     n_slots = 2 * n_seq + 2 + sum(lag for _, lag in stages)
 
     def slot(s, carry):
-        @pl.when(s == 1)
+        @pl.when(s == 2)
         def _():
             in_copy(1).wait()
             norm_half(1)
 
-        @pl.when((s >= 2) & (s < 2 + n_share))
-        def _():
-            share_tile(s - 2)
-
-        @pl.when((s >= 4) & (s < 4 + n_share))
-        def _():
-            take_tile(s - 4)
+        @pl.when((s >= 3) & (s < 3 + n_share))
+        def _():
+            share_tile(s - 3)
+
+        @pl.when((s >= 5) & (s < 5 + n_share))
+        def _():
+            take_tile(s - 5)
 
         @pl.when(s < 2 * n_seq + 2)
         def _():
@@ -536,9 +540,9 @@
             t = s - after
             after -= lag
 
-            @pl.when((t >= 0) & (t % 2 == 0) & (t < 2 * n_seq))
+            @pl.when((t == -2) | ((t > 0) & (t % 2 == 0) & (t < 2 * n_seq)))
             def _():
-                stage_fn(t // 2)
+                stage_fn(jnp.maximum(t, 0) // 2)
 
         return carry
 

time: 108 us -> 109 us (level)
  Pallas kernels: 107 us -> 109 us
where the time goes in v10:
time: 109 us
  Pallas kernels  109 us (100%)
    pallas_call x1, Pallas kernels, block(): pl.pallas_call(functools.partial(block_kernel, tile=tile), out_shape=(plt...  106 us
    pallas_call x1, Pallas kernels, store(): pl.pallas_call(store_kernel, out_shape=tuple((jax.ShapeDtypeStruct(a.shap...  2.19 us

profile of v10, /device:TPU:1, one launch (start us, length us, event | category | flops | bytes accessed | tf_op | source)
XLA Modules:
  0.0 109.2 jit_solution(9922202063367694589)
XLA Ops:
  0.6 106.3 %block.1 = (bf16[512,4096]{1,0:T(8,128)(2,1)S(1)}, bf16[1024,128]{1,0:T(8,128)(2,1)S(1)}, bf16[1024,128]{1,0:T(8,128)(2,1)S(1)}) custom-call(s32[8]{0:T(128)} %len_ref.1, bf16[4096]{0:T(1024)(128)(2,1)} %gain.1, bf16[128]{0:T(256)(128)(2,1)} %q_gain.1, bf16[128]{0:T(256)(128)(2,1)} %k_gain.1, f32[1,128]{1,0:T(1,128)} %constant.2.clone.freq, ...), custom_call_target="tpu_custom_call" | custom-call | flops 17179869184 | bytes 62914560 | tf_op jit(solution)/shard_map/block/pallas_call | solution.py:599
  107.0 2.2 %store.1 = (bf16[512,4096]{1,0:T(8,128)(2,1)}, bf16[1024,128]{1,0:T(8,128)(2,1)}, bf16[1024,128]{1,0:T(8,128)(2,1)}) custom-call(bf16[512,4096]{1,0:T(8,128)(2,1)S(1)} %get-tuple-element.9.out_in, bf16[1024,128]{1,0:T(8,128)(2,1)S(1)} %get-tuple-element.10.k_in, bf16[1024,128]{1,0:T(8,128)(2,1)S(1)} %get-tuple-element.11.v_in), custom_call_target="tpu_custom_call" | custom-call | tf_op jit(solution)/shard_map/store/pallas_call | solution.py:671
